TPU v7x, 8 devices: a whole 2x2x1 slice. The times are simulated.
8 devices in a mesh: dp: 2 (over z, y), sp: 4 (over x, core).
Axes of the slice: x: 2, y: 2, z: 1, core: 2. Of those that a mesh axis runs over, the one named last changes fastest.
Arguments:
- signal: bfloat16 [4, 1024, 512], P('dp', 'sp'), parts along dimension 0
- cond_feats: bfloat16 [4, 1024, 256], P('dp', 'sp'), parts along dimension 0
- w_now: bfloat16 [10, 512, 1024], replicated
- w_past: bfloat16 [10, 512, 1024], replicated
- w_cond: bfloat16 [10, 256, 1024], replicated
- b_gate: float32 [10, 1024], replicated
- w_res: bfloat16 [10, 512, 512], replicated
- w_skip: bfloat16 [10, 512, 256], replicated
Outputs:
- output 1: float32 [4, 1024, 512], P('dp', 'sp'), parts along dimension 0
- output 2: float32 [4, 1024, 256], P('dp', 'sp'), parts along dimension 0
There are 2 independent parts. A program takes and returns all parts, laid end to end along the dimension named above; an argument that names none is the same for every part.
All inputs are finite; a program needn't handle non-finite values.
Results may differ from a plain program's by a relative error of at most 0.00641958.
Values are sent between devices in bfloat16 or wider.
A program may use at most 1 GiB of HBM per device.

v0:
```python
import jax
import jax.numpy as jnp
from jax import lax
from jax.sharding import PartitionSpec as P


def solution(mesh):
    seq_devs = mesh.shape['sp']

    def local_stack(signal, cond_feats, w_now, w_past, w_cond, b_gate, w_res, w_skip):
        batch, span_len, channels = signal.shape
        resid = signal.astype(jnp.float32)
        skip_sum = jnp.zeros((batch, span_len, w_skip.shape[2]), jnp.float32)
        for layer in range(w_now.shape[0]):
            dilation = 2 ** layer
            now_in = resid.astype(jnp.bfloat16)
            if dilation < span_len:
                edge_rows = lax.ppermute(now_in[:, span_len - dilation:], 'sp', [(src, src + 1) for src in range(seq_devs - 1)])
                past_in = jnp.concatenate([edge_rows, now_in[:, :span_len - dilation]], axis=1)
            else:
                hop_count = dilation // span_len
                past_in = lax.ppermute(now_in, 'sp', [(src, src + hop_count) for src in range(seq_devs - hop_count)])
            gate_pre = (jnp.einsum('bsc,cg->bsg', now_in, w_now[layer], preferred_element_type=jnp.float32)
                        + jnp.einsum('bsc,cg->bsg', past_in, w_past[layer], preferred_element_type=jnp.float32)
                        + jnp.einsum('bsc,cg->bsg', cond_feats, w_cond[layer], preferred_element_type=jnp.float32)
                        + b_gate[layer])
            gated = (jnp.tanh(gate_pre[..., :channels]) * jax.nn.sigmoid(gate_pre[..., channels:])).astype(jnp.bfloat16)
            resid = resid + jnp.einsum('bsc,cd->bsd', gated, w_res[layer], preferred_element_type=jnp.float32)
            skip_sum = skip_sum + jnp.einsum('bsc,cd->bsd', gated, w_skip[layer], preferred_element_type=jnp.float32)
        return resid, skip_sum

    seq_spec = P('dp', 'sp', None)
    return jax.shard_map(local_stack, mesh=mesh,
                         in_specs=(seq_spec, seq_spec, P(), P(), P(), P(), P(), P()),
                         out_specs=(seq_spec, seq_spec), check_vma=False)
```

profile of v0, /device:TPU:0, one launch (start us, length us, event | category | flops | bytes accessed | tf_op | source)
XLA Modules:
  0.0 106.2 jit_solution(7716782701838381662)
XLA Ops:
  0.6 0.8 slice.289
  1.4 2.8 %collective-permute-start = (bf16[2,1,512]{2,1,0:T(2,128)(2,1)S(1)}, bf16[2,1,512]{2,1,0:T(2,128)(2,1)S(1)}, u32[]{:S(2)}, u32[]{:S(2)}) collective-permute-start(bf16[2,1,512]{2,1,0:T(2,128)(2,1)S(1)} %slice.289), channel_id=1, source_target_pairs={{0,1},{1,2},{2,3},{4,5},{5,6},{6,7}} | collective-permute-start | bytes 6152 | tf_op jit(solution)/shard_map/ppermute | solution.py:18
  4.2 1.6 %fusion.152 = f32[2,256,1024]{2,1,0:T(8,128)S(1)} fusion(bf16[2,256,256]{2,1,0:T(8,128)(2,1)S(1)} %copy-done, bf16[10,256,1024]{2,1,0:T(8,128)(2,1)} %param.12), kind=kOutput, calls=%fused_computation.201 | convolution fusion | flops 268435456 | bytes 2883584 | tf_op jit(solution)/shard_map/bsc,cg->bsg/dot_general | solution.py:25
  5.8 1.6 %fusion.149 = f32[2,256,1024]{2,1,0:T(8,128)S(1)} fusion(bf16[2,256,256]{2,1,0:T(8,128)(2,1)S(1)} %copy-done, bf16[10,256,1024]{2,1,0:T(8,128)(2,1)} %param.12), kind=kOutput, calls=%fused_computation.198 | convolution fusion | flops 268435456 | bytes 2883584 | tf_op jit(solution)/shard_map/bsc,cg->bsg/dot_general | solution.py:25
  7.5 1.6 %fusion.146 = f32[2,256,1024]{2,1,0:T(8,128)S(1)} fusion(bf16[2,256,256]{2,1,0:T(8,128)(2,1)S(1)} %copy-done, bf16[10,256,1024]{2,1,0:T(8,128)(2,1)} %param.12), kind=kOutput, calls=%fused_computation.195 | convolution fusion | flops 268435456 | bytes 2883584 | tf_op jit(solution)/shard_map/bsc,cg->bsg/dot_general | solution.py:25
  9.1 1.6 %fusion.143 = f32[2,256,1024]{2,1,0:T(8,128)S(1)} fusion(bf16[2,256,256]{2,1,0:T(8,128)(2,1)S(1)} %copy-done, bf16[10,256,1024]{2,1,0:T(8,128)(2,1)} %param.12), kind=kOutput, calls=%fused_computation.192 | convolution fusion | flops 268435456 | bytes 2883584 | tf_op jit(solution)/shard_map/bsc,cg->bsg/dot_general | solution.py:25
  10.8 0.4 fusion.140
  11.2 0.4 fusion.137
  11.7 0.4 fusion.134
  12.2 0.4 fusion.131
  12.6 0.4 fusion.128
  13.1 0.4 fusion.125
  13.5 0.4 slice-done.2
  14.4 0.7 fusion.68
  15.3 0.8 add_add_fusion.9
  16.1 0.4 fusion.90
  16.5 1.5 %fusion.205 = (bf16[2,256,512]{2,1,0:T(8,128)(2,1)S(1)}, f32[2,256,512]{2,1,0:T(8,128)S(1)}) fusion(bf16[2,256,512]{2,1,0:T(8,128)(2,1)S(1)} %fusion.90, bf16[10,512,512]{2,1,0:T(8,128)(2,1)} %param.14, bf16[2,256,512]{2,1,0:T(8,128)(2,1)S(1)} %copy-done.3), kind=kOutput, calls=%fused_computation.254 | convolution fusion | flops 269221888 | bytes 3145728 | tf_op jit(solution)/shard_map/bsc,cd->bsd/dot_general | solution.py:28
  18.0 0.7 fusion.65
  18.8 4.5 %collective-permute-start.1 = (bf16[2,2,512]{2,1,0:T(2,128)(2,1)S(1)}, bf16[2,2,512]{2,1,0:T(2,128)(2,1)S(1)}, u32[]{:S(2)}, u32[]{:S(2)}) collective-permute-start(bf16[2,2,512]{2,1,0:T(2,128)(2,1)S(1)} %slice.386), channel_id=1, source_target_pairs={{0,1},{1,2},{2,3},{4,5},{5,6},{6,7}} | collective-permute-start | bytes 12296 | tf_op jit(solution)/shard_map/ppermute | solution.py:18
  23.3 1.2 %fusion.183 = f32[2,256,256]{2,1,0:T(8,128)S(1)} fusion(bf16[2,256,512]{2,1,0:T(8,128)(2,1)S(1)} %fusion.90, bf16[10,512,256]{2,1,0:T(8,128)(2,1)} %param.15), kind=kOutput, calls=%fused_computation.232 | convolution fusion | flops 134217728 | bytes 1310720 | tf_op jit(solution)/shard_map/bsc,cd->bsd/dot_general | solution.py:29
  24.5 0.8 add_add_fusion.8
  25.7 2.5 %fusion.206 = (bf16[2,256,512]{2,1,0:T(8,128)(2,1)S(1)}, f32[2,256,512]{2,1,0:T(8,128)}) fusion(f32[2,256,512]{2,1,0:T(8,128)S(1)} %get-tuple-element.15, bf16[2,256,512]{2,1,0:T(8,128)(2,1)S(1)} %fusion.91, bf16[10,512,512]{2,1,0:T(8,128)(2,1)} %param.14), kind=kOutput, calls=%fused_computation.255 | convolution fusion | flops 268959744 | bytes 3670016 | tf_op jit(solution)/shard_map/bsc,cd->bsd/dot_general | solution.py:28
  28.2 0.7 fusion.62
  29.0 1.9 %collective-permute-start.2 = (bf16[2,4,512]{2,1,0:T(4,128)(2,1)S(1)}, bf16[2,4,512]{2,1,0:T(4,128)(2,1)S(1)}, u32[]{:S(2)}, u32[]{:S(2)}) collective-permute-start(bf16[2,4,512]{2,1,0:T(4,128)(2,1)S(1)} %slice.390), channel_id=1, source_target_pairs={{0,1},{1,2},{2,3},{4,5},{5,6},{6,7}} | collective-permute-start | bytes 24584 | tf_op jit(solution)/shard_map/ppermute | solution.py:18
  30.9 2.2 %convolution_add_fusion.18 = f32[2,256,256]{2,1,0:T(8,128)} fusion(f32[2,256,256]{2,1,0:T(8,128)S(1)} %fusion.183, bf16[2,256,512]{2,1,0:T(8,128)(2,1)S(1)} %fusion.91, bf16[10,512,256]{2,1,0:T(8,128)(2,1)} %param.15), kind=kOutput, calls=%fused_computation.28 | convolution fusion | flops 134348800 | bytes 1835008 | tf_op jit(solution)/shard_map/bsc,cd->bsd/dot_general | solution.py:29
  33.1 0.8 add_add_fusion.7
  34.4 0.8 copy-done.4
  35.2 0.4 fusion.207
  35.7 0.7 fusion.59
  36.4 3.8 %collective-permute-start.3 = (bf16[2,8,512]{2,1,0:T(8,128)(2,1)S(1)}, bf16[2,8,512]{2,1,0:T(8,128)(2,1)S(1)}, u32[]{:S(2)}, u32[]{:S(2)}) collective-permute-start(bf16[2,8,512]{2,1,0:T(8,128)(2,1)S(1)} %slice.394), channel_id=1, source_target_pairs={{0,1},{1,2},{2,3},{4,5},{5,6},{6,7}} | collective-permute-start | bytes 49160 | tf_op jit(solution)/shard_map/ppermute | solution.py:18
  40.2 1.2 %convolution_add_fusion.17 = f32[2,256,256]{2,1,0:T(8,128)S(1)} fusion(f32[2,256,256]{2,1,0:T(8,128)S(1)} %copy-done.6, bf16[2,256,512]{2,1,0:T(8,128)(2,1)S(1)} %fusion.92, bf16[10,512,256]{2,1,0:T(8,128)(2,1)} %param.15), kind=kOutput, calls=%fused_computation.27 | convolution fusion | flops 134348800 | bytes 1835008 | tf_op jit(solution)/shard_map/bsc,cd->bsd/dot_general | solution.py:29
  41.5 0.8 add_add_fusion.6
  42.7 0.4 fusion.208
  43.2 0.7 fusion.56
  43.9 2.7 %collective-permute-start.4 = (bf16[2,16,512]{2,1,0:T(8,128)(2,1)S(1)}, bf16[2,16,512]{2,1,0:T(8,128)(2,1)S(1)}, u32[]{:S(2)}, u32[]{:S(2)}) collective-permute-start(bf16[2,16,512]{2,1,0:T(8,128)(2,1)S(1)} %slice.398), channel_id=1, source_target_pairs={{0,1},{1,2},{2,3},{4,5},{5,6},{6,7}} | collective-permute-start | bytes 98312 | tf_op jit(solution)/shard_map/ppermute | solution.py:18
  46.7 1.2 %convolution_add_fusion.16 = f32[2,256,256]{2,1,0:T(8,128)S(1)} fusion(f32[2,256,256]{2,1,0:T(8,128)S(1)} %convolution_add_fusion.17, bf16[2,256,512]{2,1,0:T(8,128)(2,1)S(1)} %fusion.93, bf16[10,512,256]{2,1,0:T(8,128)(2,1)} %param.15), kind=kOutput, calls=%fused_computation.26 | convolution fusion | flops 134348800 | bytes 1835008 | tf_op jit(solution)/shard_map/bsc,cd->bsd/dot_general | solution.py:29
  48.0 0.8 add_add_fusion.5
  49.2 0.4 fusion.209
  49.6 0.7 fusion.53
  50.3 3.6 %collective-permute-start.5 = (bf16[2,32,512]{2,1,0:T(8,128)(2,1)S(1)}, bf16[2,32,512]{2,1,0:T(8,128)(2,1)S(1)}, u32[]{:S(2)}, u32[]{:S(2)}) collective-permute-start(bf16[2,32,512]{2,1,0:T(8,128)(2,1)S(1)} %slice.402), channel_id=1, source_target_pairs={{0,1},{1,2},{2,3},{4,5},{5,6},{6,7}} | collective-permute-start | bytes 196616 | tf_op jit(solution)/shard_map/ppermute | solution.py:18
  53.9 1.2 %convolution_add_fusion.15 = f32[2,256,256]{2,1,0:T(8,128)S(1)} fusion(f32[2,256,256]{2,1,0:T(8,128)S(1)} %convolution_add_fusion.16, bf16[2,256,512]{2,1,0:T(8,128)(2,1)S(1)} %fusion.94, bf16[10,512,256]{2,1,0:T(8,128)(2,1)} %param.15), kind=kOutput, calls=%fused_computation.25 | convolution fusion | flops 134348800 | bytes 1835008 | tf_op jit(solution)/shard_map/bsc,cd->bsd/dot_general | solution.py:29
  55.2 0.8 add_add_fusion.4
  56.4 0.4 fusion.210
  56.9 0.7 fusion.50
  57.6 4.1 %collective-permute-start.6 = (bf16[2,64,512]{2,1,0:T(8,128)(2,1)S(1)}, bf16[2,64,512]{2,1,0:T(8,128)(2,1)S(1)}, u32[]{:S(2)}, u32[]{:S(2)}) collective-permute-start(bf16[2,64,512]{2,1,0:T(8,128)(2,1)S(1)} %slice.406), channel_id=1, source_target_pairs={{0,1},{1,2},{2,3},{4,5},{5,6},{6,7}} | collective-permute-start | bytes 393224 | tf_op jit(solution)/shard_map/ppermute | solution.py:18
  62.0 0.6 collective-permute-done.6
  62.7 0.7 add_add_fusion.3
  63.8 0.4 fusion.211
  64.3 0.7 fusion.47
  65.0 5.2 %collective-permute-start.7 = (bf16[2,128,512]{2,1,0:T(8,128)(2,1)S(1)}, bf16[2,128,512]{2,1,0:T(8,128)(2,1)S(1)}, u32[]{:S(2)}, u32[]{:S(2)}) collective-permute-start(bf16[2,128,512]{2,1,0:T(8,128)(2,1)S(1)} %get-tuple-element.2), channel_id=1, source_target_pairs={{0,1},{1,2},{2,3},{4,5},{5,6},{6,7}} | collective-permute-start | bytes 786440 | tf_op jit(solution)/shard_map/ppermute | solution.py:18
  70.6 0.8 collective-permute-done.7
  71.4 0.7 add_add_fusion.2
  72.6 0.4 fusion.212
  73.0 6.5 %collective-permute-start.8 = (bf16[2,256,512]{2,1,0:T(8,128)(2,1)S(1)}, bf16[2,256,512]{2,1,0:T(8,128)(2,1)S(1)}, u32[]{:S(2)}, u32[]{:S(2)}) collective-permute-start(bf16[2,256,512]{2,1,0:T(8,128)(2,1)S(1)} %get-tuple-element.28), channel_id=1, source_target_pairs={{0,1},{1,2},{2,3},{4,5},{5,6},{6,7}} | collective-permute-start | bytes 1572872 | tf_op jit(solution)/shard_map/ppermute | solution.py:22
  79.8 0.7 fusion.44
  80.6 0.5 collective-permute-done.8
  81.0 0.7 add_add_fusion.1
  82.2 0.4 fusion.213
  82.6 11.4 %collective-permute-start.9 = (bf16[2,256,512]{2,1,0:T(8,128)(2,1)S(1)}, bf16[2,256,512]{2,1,0:T(8,128)(2,1)S(1)}, u32[]{:S(2)}, u32[]{:S(2)}) collective-permute-start(bf16[2,256,512]{2,1,0:T(8,128)(2,1)S(1)} %get-tuple-element.30), channel_id=1, source_target_pairs={{0,2},{1,3},{4,6},{5,7}} | collective-permute-start | bytes 1572872 | tf_op jit(solution)/shard_map/ppermute | solution.py:22
  94.3 0.7 fusion.41
  95.0 7.5 %collective-permute-done.9 = bf16[2,256,512]{2,1,0:T(8,128)(2,1)S(1)} collective-permute-done((bf16[2,256,512]{2,1,0:T(8,128)(2,1)S(1)}, bf16[2,256,512]{2,1,0:T(8,128)(2,1)S(1)}, u32[]{:S(2)}, u32[]{:S(2)}) %collective-permute-start.9) | collective-permute-done | bytes 524320 | tf_op jit(solution)/shard_map/ppermute | solution.py:22
  102.6 0.7 add_add_fusion
  103.7 1.1 %convolution_add_fusion.10 = f32[2,256,256]{2,1,0:T(8,128)} fusion(f32[2,256,256]{2,1,0:T(8,128)S(1)} %convolution_add_fusion.11, bf16[2,256,512]{2,1,0:T(8,128)(2,1)S(1)} %fusion.99, bf16[10,512,256]{2,1,0:T(8,128)(2,1)S(1)} %copy-done.5), kind=kOutput, calls=%fused_computation.20 | convolution fusion | flops 134348800 | bytes 1835008 | tf_op jit(solution)/shard_map/bsc,cd->bsd/dot_general | solution.py:29
  104.8 1.4 %convolution_add_fusion = f32[2,256,512]{2,1,0:T(8,128)} fusion(f32[2,256,512]{2,1,0:T(8,128)S(1)} %get-tuple-element.31, bf16[2,256,512]{2,1,0:T(8,128)(2,1)S(1)} %fusion.99, bf16[10,512,512]{2,1,0:T(8,128)(2,1)S(1)} %bitcast.278), kind=kOutput, calls=%fused_computation.10 | convolution fusion | flops 268697600 | bytes 3145728 | tf_op jit(solution)/shard_map/bsc,cd->bsd/dot_general | solution.py:28
  (64 shorter events, 5.9 us)
Async XLA Ops:
  0.6 3.5 %copy-start = (bf16[2,256,256]{2,1,0:T(8,128)(2,1)S(1)}, bf16[2,256,256]{2,1,0:T(8,128)(2,1)}, u32[]{:S(2)}) copy-start(bf16[2,256,256]{2,1,0:T(8,128)(2,1)} %param.9) | copy-start | bytes 786436
  1.4 13.8 %collective-permute-start = (bf16[2,1,512]{2,1,0:T(2,128)(2,1)S(1)}, bf16[2,1,512]{2,1,0:T(2,128)(2,1)S(1)}, u32[]{:S(2)}, u32[]{:S(2)}) collective-permute-start(bf16[2,1,512]{2,1,0:T(2,128)(2,1)S(1)} %slice.289), channel_id=1, source_target_pairs={{0,1},{1,2},{2,3},{4,5},{5,6},{6,7}} | collective-permute-start | bytes 6152 | tf_op jit(solution)/shard_map/ppermute | solution.py:18
  4.2 11.1 %slice-start.3 = ((s8[10485760]{0:T(1024)(128)(4,1)}), s8[4194304]{0:T(1024)(128)(4,1)S(1)}, s32[]{:S(2)}) async-start(s8[10485760]{0:T(1024)(128)(4,1)} %bitcast.275), calls=%async_computation.3 | async-start | bytes 8388608
  5.8 4.9 %copy-start.2 = (bf16[10,256,1024]{2,1,0:T(8,128)(2,1)S(1)}, bf16[10,256,1024]{2,1,0:T(8,128)(2,1)}, u32[]{:S(2)}) copy-start(bf16[10,256,1024]{2,1,0:T(8,128)(2,1)} %param.12) | copy-start | bytes 15728644
  7.5 6.0 %slice-start = ((s8[10485760]{0:T(1024)(128)(4,1)}), s8[4194304]{0:T(1024)(128)(4,1)S(1)}, s32[]{:S(2)}) async-start(s8[10485760]{0:T(1024)(128)(4,1)} %bitcast.273), calls=%async_computation | async-start | bytes 8388608
  9.1 6.2 %slice-start.4 = ((s8[10485760]{0:T(1024)(128)(4,1)}), s8[4194304]{0:T(1024)(128)(4,1)S(1)}, s32[]{:S(2)}) async-start(s8[10485760]{0:T(1024)(128)(4,1)} %bitcast.275), calls=%async_computation.4 | async-start | bytes 8388608
  10.8 2.7 %slice-start.1 = ((s8[10485760]{0:T(1024)(128)(4,1)}), s8[4194304]{0:T(1024)(128)(4,1)S(1)}, s32[]{:S(2)}) async-start(s8[10485760]{0:T(1024)(128)(4,1)} %bitcast.273), calls=%async_computation.1 | async-start | bytes 8388608
  12.1 1.8 %slice-start.2 = ((s8[10485760]{0:T(1024)(128)(4,1)}), s8[2097152]{0:T(1024)(128)(4,1)S(1)}, s32[]{:S(2)}) async-start(s8[10485760]{0:T(1024)(128)(4,1)} %bitcast.273), calls=%async_computation.2 | async-start | bytes 4194304
  12.2 3.1 %slice-start.5 = ((s8[10485760]{0:T(1024)(128)(4,1)}), s8[2097152]{0:T(1024)(128)(4,1)S(1)}, s32[]{:S(2)}) async-start(s8[10485760]{0:T(1024)(128)(4,1)} %bitcast.275), calls=%async_computation.5 | async-start | bytes 4194304
  13.1 1.3 %copy-start.3 = (bf16[2,256,512]{2,1,0:T(8,128)(2,1)S(1)}, bf16[2,256,512]{2,1,0:T(8,128)(2,1)}, u32[]{:S(2)}) copy-start(bf16[2,256,512]{2,1,0:T(8,128)(2,1)} %param.8) | copy-start | bytes 1572868
  14.4 0.8 copy-start.7
  18.8 5.8 %collective-permute-start.1 = (bf16[2,2,512]{2,1,0:T(2,128)(2,1)S(1)}, bf16[2,2,512]{2,1,0:T(2,128)(2,1)S(1)}, u32[]{:S(2)}, u32[]{:S(2)}) collective-permute-start(bf16[2,2,512]{2,1,0:T(2,128)(2,1)S(1)} %slice.386), channel_id=1, source_target_pairs={{0,1},{1,2},{2,3},{4,5},{5,6},{6,7}} | collective-permute-start | bytes 12296 | tf_op jit(solution)/shard_map/ppermute | solution.py:18
  29.0 4.1 %collective-permute-start.2 = (bf16[2,4,512]{2,1,0:T(4,128)(2,1)S(1)}, bf16[2,4,512]{2,1,0:T(4,128)(2,1)S(1)}, u32[]{:S(2)}, u32[]{:S(2)}) collective-permute-start(bf16[2,4,512]{2,1,0:T(4,128)(2,1)S(1)} %slice.390), channel_id=1, source_target_pairs={{0,1},{1,2},{2,3},{4,5},{5,6},{6,7}} | collective-permute-start | bytes 24584 | tf_op jit(solution)/shard_map/ppermute | solution.py:18
  30.9 3.4 %slice-start.6 = ((s8[5242880]{0:T(1024)(128)(4,1)}), s8[4194304]{0:T(1024)(128)(4,1)S(1)}, s32[]{:S(2)}) async-start(s8[5242880]{0:T(1024)(128)(4,1)} %bitcast.277), calls=%async_computation.6 | async-start | bytes 8388608
  33.1 1.2 %slice-start.7 = ((s8[5242880]{0:T(1024)(128)(4,1)}), s8[1048576]{0:T(1024)(128)(4,1)S(1)}, s32[]{:S(2)}) async-start(s8[5242880]{0:T(1024)(128)(4,1)} %bitcast.277), calls=%async_computation.7 | async-start | bytes 2097152
  33.9 1.3 %copy-start.4 = (f32[2,256,512]{2,1,0:T(8,128)S(1)}, f32[2,256,512]{2,1,0:T(8,128)}, u32[]{:S(2)}) copy-start(f32[2,256,512]{2,1,0:T(8,128)} %get-tuple-element.17) | copy-start | bytes 3145732
  35.6 4.6 %copy-start.6 = (f32[2,256,256]{2,1,0:T(8,128)S(1)}, f32[2,256,256]{2,1,0:T(8,128)}, u32[]{:S(2)}) copy-start(f32[2,256,256]{2,1,0:T(8,128)} %convolution_add_fusion.18) | copy-start | bytes 1572868
  36.4 5.1 %collective-permute-start.3 = (bf16[2,8,512]{2,1,0:T(8,128)(2,1)S(1)}, bf16[2,8,512]{2,1,0:T(8,128)(2,1)S(1)}, u32[]{:S(2)}, u32[]{:S(2)}) collective-permute-start(bf16[2,8,512]{2,1,0:T(8,128)(2,1)S(1)} %slice.394), channel_id=1, source_target_pairs={{0,1},{1,2},{2,3},{4,5},{5,6},{6,7}} | collective-permute-start | bytes 49160 | tf_op jit(solution)/shard_map/ppermute | solution.py:18
  43.9 4.0 %collective-permute-start.4 = (bf16[2,16,512]{2,1,0:T(8,128)(2,1)S(1)}, bf16[2,16,512]{2,1,0:T(8,128)(2,1)S(1)}, u32[]{:S(2)}, u32[]{:S(2)}) collective-permute-start(bf16[2,16,512]{2,1,0:T(8,128)(2,1)S(1)} %slice.398), channel_id=1, source_target_pairs={{0,1},{1,2},{2,3},{4,5},{5,6},{6,7}} | collective-permute-start | bytes 98312 | tf_op jit(solution)/shard_map/ppermute | solution.py:18
  50.3 4.9 %collective-permute-start.5 = (bf16[2,32,512]{2,1,0:T(8,128)(2,1)S(1)}, bf16[2,32,512]{2,1,0:T(8,128)(2,1)S(1)}, u32[]{:S(2)}, u32[]{:S(2)}) collective-permute-start(bf16[2,32,512]{2,1,0:T(8,128)(2,1)S(1)} %slice.402), channel_id=1, source_target_pairs={{0,1},{1,2},{2,3},{4,5},{5,6},{6,7}} | collective-permute-start | bytes 196616 | tf_op jit(solution)/shard_map/ppermute | solution.py:18
  56.9 4.8 %copy-start.5 = (bf16[10,512,256]{2,1,0:T(8,128)(2,1)S(1)}, bf16[10,512,256]{2,1,0:T(8,128)(2,1)}, u32[]{:S(2)}) copy-start(bf16[10,512,256]{2,1,0:T(8,128)(2,1)} %param.15) | copy-start | bytes 7864324
  57.6 5.0 %collective-permute-start.6 = (bf16[2,64,512]{2,1,0:T(8,128)(2,1)S(1)}, bf16[2,64,512]{2,1,0:T(8,128)(2,1)S(1)}, u32[]{:S(2)}, u32[]{:S(2)}) collective-permute-start(bf16[2,64,512]{2,1,0:T(8,128)(2,1)S(1)} %slice.406), channel_id=1, source_target_pairs={{0,1},{1,2},{2,3},{4,5},{5,6},{6,7}} | collective-permute-start | bytes 393224 | tf_op jit(solution)/shard_map/ppermute | solution.py:18
  65.0 6.4 %collective-permute-start.7 = (bf16[2,128,512]{2,1,0:T(8,128)(2,1)S(1)}, bf16[2,128,512]{2,1,0:T(8,128)(2,1)S(1)}, u32[]{:S(2)}, u32[]{:S(2)}) collective-permute-start(bf16[2,128,512]{2,1,0:T(8,128)(2,1)S(1)} %get-tuple-element.2), channel_id=1, source_target_pairs={{0,1},{1,2},{2,3},{4,5},{5,6},{6,7}} | collective-permute-start | bytes 786440 | tf_op jit(solution)/shard_map/ppermute | solution.py:18
  73.0 8.0 %collective-permute-start.8 = (bf16[2,256,512]{2,1,0:T(8,128)(2,1)S(1)}, bf16[2,256,512]{2,1,0:T(8,128)(2,1)S(1)}, u32[]{:S(2)}, u32[]{:S(2)}) collective-permute-start(bf16[2,256,512]{2,1,0:T(8,128)(2,1)S(1)} %get-tuple-element.28), channel_id=1, source_target_pairs={{0,1},{1,2},{2,3},{4,5},{5,6},{6,7}} | collective-permute-start | bytes 1572872 | tf_op jit(solution)/shard_map/ppermute | solution.py:22
  82.6 20.0 %collective-permute-start.9 = (bf16[2,256,512]{2,1,0:T(8,128)(2,1)S(1)}, bf16[2,256,512]{2,1,0:T(8,128)(2,1)S(1)}, u32[]{:S(2)}, u32[]{:S(2)}) collective-permute-start(bf16[2,256,512]{2,1,0:T(8,128)(2,1)S(1)} %get-tuple-element.30), channel_id=1, source_target_pairs={{0,2},{1,3},{4,6},{5,7}} | collective-permute-start | bytes 1572872 | tf_op jit(solution)/shard_map/ppermute | solution.py:22
  103.3 2.9 %copy-start.1 = (bf16[2,256,256]{2,1,0:T(8,128)(2,1)S(1)}, bf16[2,256,256]{2,1,0:T(8,128)(2,1)}, u32[]{:S(2)}) copy-start(bf16[2,256,256]{2,1,0:T(8,128)(2,1)} %param.9) | copy-start | bytes 786436
where the time goes:
time: 107 us; the launch traced here: 106 us
  starting transfers between devices  46.5 us (43%)
  matrix products  41.8 us (39%)
  waiting for transfers between devices  9.45 us (9%)
  other arithmetic  4.25 us (4%)
  local copies, waits for them, and re-layouts  2.89 us (3%)
  between operations  1.4 us (1%)
    ppermute x8, starting transfers between devices, local_stack(): lax.ppermute(now_in[:, span_len - dilation:], 'sp', [(src, src + 1) for s...  28.6 us
    ppermute x2, starting transfers between devices, local_stack(): lax.ppermute(now_in, 'sp', [(src, src + hop_count) for src in range(seq_d...  17.9 us
    dot_general x10, matrix products, local_stack(): jnp.einsum('bsc,cd->bsd', gated, w_skip[layer], preferred_element_type=jn...  9.45 us
    dot_general x10, matrix products, local_stack(): jnp.einsum('bsc,cg->bsg', cond_feats, w_cond[layer], preferred_element_ty...  9.17 us
    dot_general x10, matrix products, local_stack(): jnp.einsum('bsc,cd->bsd', gated, w_res[layer], preferred_element_type=jnp...  8.44 us
    ppermute x2, waiting for transfers between devices, local_stack(): lax.ppermute(now_in, 'sp', [(src, src + hop_count) for src in range(seq_d...  8 us
    dot_general x10, matrix products, local_stack(): jnp.einsum('bsc,cg->bsg', past_in, w_past[layer], preferred_element_type=...  7.51 us
    dot_general x10, matrix products, local_stack(): jnp.einsum('bsc,cg->bsg', now_in, w_now[layer], preferred_element_type=jn...  7.19 us
  transfers between devices with their start and end apart: 10, of which 4 were waited for; matrix products, arithmetic and copies ran while one was open for 19% of the time, Pallas kernels for 0%

commit v1 on v0

v1 whole, which is shorter than its diff:
```python
import functools

import jax
import jax.numpy as jnp
from jax import lax
from jax.experimental import pallas as pl
from jax.experimental.pallas import tpu as pltpu
from jax.sharding import PartitionSpec as P

BF16, F32 = jnp.bfloat16, jnp.float32
MESH = pl.DeviceIdType.MESH
AHEAD = 3


def stack_kernel(n_sp, signal, cond, w_now, w_past, w_cond, b_gate, w_res, w_skip, h_out, skip_out,
                 u, c, bias, w_in, w_mix, h, skip,
                 sig_sem, cond_sem, bias_sem, w_sem, send_sem, recv_sem, out_sem):
    batch, layers, two_span, ch = u.shape
    span = two_span // 2
    cond_ch = c.shape[2]
    dp, me = lax.axis_index('dp'), lax.axis_index('sp')

    def weight_copies(layer):
        pairs = (
            (w_now.at[layer], w_in.at[layer, pl.ds(0, ch)]),
            (w_cond.at[layer], w_in.at[layer, pl.ds(ch, cond_ch)]),
            (w_past.at[layer], w_in.at[layer, pl.ds(ch + cond_ch, ch)]),
            (w_res.at[layer], w_mix.at[layer, :, pl.ds(0, ch)]),
            (w_skip.at[layer], w_mix.at[layer, :, pl.ds(ch, skip.shape[2])]),
        )
        return [pltpu.make_async_copy(src, dst, w_sem.at[layer, i]) for i, (src, dst) in enumerate(pairs)]

    def hops(layer):
        return max(1, 2 ** layer // span)

    def halo(layer):
        return min(max(16, 2 ** layer), span)

    def edge_copy(s, layer):
        rows = halo(layer)
        return pltpu.make_async_remote_copy(
            src_ref=u.at[s, layer, pl.ds(2 * span - rows, rows)],
            dst_ref=u.at[s, layer, pl.ds(span - rows, rows)],
            send_sem=send_sem.at[s, layer], recv_sem=recv_sem.at[s, layer],
            device_id=(dp, lax.rem(me + hops(layer), n_sp)), device_id_type=MESH)

    def send_edge(s, layer):
        @pl.when(me + hops(layer) < n_sp)
        def _():
            edge_copy(s, layer).start()

    sig_in = [pltpu.make_async_copy(signal.at[s], u.at[s, 0, pl.ds(span, span)], sig_sem.at[s]) for s in range(batch)]
    cond_in = [pltpu.make_async_copy(cond.at[s], c.at[s], cond_sem.at[s]) for s in range(batch)]
    bias_in = pltpu.make_async_copy(b_gate, bias, bias_sem)
    sig_in[0].start()
    cond_in[0].start()
    bias_in.start()
    for layer in range(AHEAD):
        for copy in weight_copies(layer):
            copy.start()
    for s in range(1, batch):
        sig_in[s].start()
        cond_in[s].start()

    barrier = pltpu.get_barrier_semaphore()
    for off in range(1, n_sp):
        pl.semaphore_signal(barrier, inc=1, device_id=(dp, lax.rem(me + off, n_sp)), device_id_type=MESH)

    for layer in range(layers):
        @pl.when(me < hops(layer))
        def _():
            rows = halo(layer)
            for s in range(batch):
                u[s, layer, span - rows:span] = jnp.zeros((rows, ch), BF16)

    pl.semaphore_wait(barrier, n_sp - 1)

    for s in range(batch):
        sig_in[s].wait()
        send_edge(s, 0)
    for s in range(batch):
        cond_in[s].wait()
    bias_in.wait()

    def step(s, layer):
        dilation = 2 ** layer

        @pl.when(s == 0)
        def _():
            if layer + AHEAD < layers:
                for copy in weight_copies(layer + AHEAD):
                    copy.start()
            for copy in weight_copies(layer):
                copy.wait()

        @pl.when(me >= hops(layer))
        def _():
            edge_copy(s, layer).wait_recv()

        now = u[s, layer, span:]
        if dilation < 16:
            wide = u[s, layer, span - 16:].astype(F32)
            past = pltpu.roll(wide, dilation, axis=0)[16:].astype(BF16)
        else:
            past = u[s, layer, span - halo(layer):2 * span - halo(layer)]
        x = jnp.concatenate([now, c[s], past], axis=1)
        half = ch // 2
        gated = []
        for i in range(2):
            lo, hi = i * half, (i + 1) * half
            zf = jnp.dot(x, w_in[layer, :, lo:hi], preferred_element_type=F32) + bias[layer:layer + 1, lo:hi]
            zg = jnp.dot(x, w_in[layer, :, ch + lo:ch + hi], preferred_element_type=F32) + bias[layer:layer + 1, ch + lo:ch + hi]
            gated.append((jnp.tanh(zf) * (0.5 * jnp.tanh(0.5 * zg) + 0.5)).astype(BF16))
        a = jnp.concatenate(gated, axis=1)
        base = now.astype(F32) if layer == 0 else h[s]
        new_h = base + jnp.dot(a, w_mix[layer, :, :ch], preferred_element_type=F32)
        h[s] = new_h
        if layer + 1 < layers:
            u[s, layer + 1, span:] = new_h.astype(BF16)
        new_skip = jnp.dot(a, w_mix[layer, :, ch:], preferred_element_type=F32)
        skip[s] = new_skip if layer == 0 else skip[s] + new_skip
        if layer + 1 < layers:
            send_edge(s, layer + 1)
        else:
            pltpu.make_async_copy(h.at[s], h_out.at[s], out_sem.at[s, 0]).start()
            pltpu.make_async_copy(skip.at[s], skip_out.at[s], out_sem.at[s, 1]).start()

    def run(i, carry):
        early = jnp.where(i < 9, i, jnp.where(i < 18, i + 1, jnp.where(i < 19, 9, 19)))
        late = jnp.where(i < 8, i, jnp.where(i < 10, i + 2, jnp.where(i < 11, 8, jnp.where(
            i < 17, i + 1, jnp.where(i < 18, 9, i)))))
        code = jnp.where(me < n_sp // 2, early, late)
        s, which = code // layers, code % layers
        for layer in range(layers):
            @pl.when(which == layer)
            def _():
                step(s, layer)
        return carry

    lax.fori_loop(0, batch * layers, run, 0)

    for s in range(batch):
        pltpu.make_async_copy(h.at[s], h_out.at[s], out_sem.at[s, 0]).wait()
        pltpu.make_async_copy(skip.at[s], skip_out.at[s], out_sem.at[s, 1]).wait()
        for layer in range(layers):
            @pl.when(me + hops(layer) < n_sp)
            def _():
                edge_copy(s, layer).wait_send()


def solution(mesh):
    n_sp = mesh.shape['sp']

    def local_stack(signal, cond_feats, w_now, w_past, w_cond, b_gate, w_res, w_skip):
        batch, span, ch = signal.shape
        layers, cond_ch, skip_ch = w_now.shape[0], cond_feats.shape[2], w_skip.shape[2]
        anywhere = pl.BlockSpec(memory_space=pl.ANY)
        return pl.pallas_call(
            functools.partial(stack_kernel, n_sp),
            out_shape=[jax.ShapeDtypeStruct((batch, span, ch), F32), jax.ShapeDtypeStruct((batch, span, skip_ch), F32)],
            in_specs=[anywhere] * 8,
            out_specs=[anywhere] * 2,
            scratch_shapes=[
                pltpu.VMEM((batch, layers, 2 * span, ch), BF16),
                pltpu.VMEM((batch, span, cond_ch), BF16),
                pltpu.VMEM((layers, 2 * ch), F32),
                pltpu.VMEM((layers, 2 * ch + cond_ch, 2 * ch), BF16),
                pltpu.VMEM((layers, ch, ch + skip_ch), BF16),
                pltpu.VMEM((batch, span, ch), F32),
                pltpu.VMEM((batch, span, skip_ch), F32),
                pltpu.SemaphoreType.DMA((batch,)),
                pltpu.SemaphoreType.DMA((batch,)),
                pltpu.SemaphoreType.DMA,
                pltpu.SemaphoreType.DMA((layers, 5)),
                pltpu.SemaphoreType.DMA((batch, layers)),
                pltpu.SemaphoreType.DMA((batch, layers)),
                pltpu.SemaphoreType.DMA((batch, 2)),
            ],
            compiler_params=pltpu.CompilerParams(collective_id=0, has_side_effects=True, vmem_limit_bytes=60 * 2 ** 20),
        )(signal, cond_feats, w_now, w_past, w_cond, b_gate, w_res, w_skip)

    seq_spec = P('dp', 'sp', None)
    return jax.shard_map(local_stack, mesh=mesh,
                         in_specs=(seq_spec, seq_spec, P(), P(), P(), P(), P(), P()),
                         out_specs=(seq_spec, seq_spec), check_vma=False)
```

time: 107 us -> 47.5 us (0.44)
  the two profiles are of different devices: /device:TPU:0 before, /device:TPU:7 now
where the time goes in v1:
time: 47.5 us; the launch traced here: 47.3 us
  Pallas kernels  42.6 us (90%)
  local copies, waits for them, and re-layouts  4.13 us (9%)
  between operations  0.64 us (1%)
    pallas_call x1, Pallas kernels, local_stack(): pl.pallas_call(functools.partial(stack_kernel, n_sp), out_shape=[jax.Shap...  42.6 us
    unnamed x2, local copies, waits for them, and re-layouts  4.13 us

profile of v1, /device:TPU:7, one launch (start us, length us, event | category | flops | bytes accessed | tf_op | source)
XLA Modules:
  0.0 47.3 jit_solution(17020229113823262537)
XLA Ops:
  0.6 42.6 %shard_map.95 = (f32[2,256,512]{2,1,0:T(8,128)}, f32[2,256,256]{2,1,0:T(8,128)}) custom-call(bf16[2,256,512]{2,1,0:T(8,128)(2,1)} %signal.1, bf16[2,256,256]{2,1,0:T(8,128)(2,1)} %cond.1, bf16[10,512,1024]{2,1,0:T(8,128)(2,1)} %w_now.1, bf16[10,512,1024]{2,1,0:T(8,128)(2,1)} %w_past.1, bf16[10,256,1024]{2,1,0:T(8,128)(2,1)} %w_cond.1, f32[10,1024]{1,0:T(8,128)} %b_gate.1, ...), custom_call_target="tpu_custom_call" | custom-call | tf_op jit(solution)/shard_map/pallas_call | solution.py:158
  43.2 2.3 %copy.12 = f32[2,256,512]{2,1,0:T(8,128)} copy(f32[2,256,512]{2,1,0:T(8,128)} %get-tuple-element.4) | data formatting | bytes 2097152
  45.5 1.9 %copy.13 = f32[2,256,256]{2,1,0:T(8,128)} copy(f32[2,256,256]{2,1,0:T(8,128)} %get-tuple-element.5) | data formatting | bytes 1048576

commit v2 on v1

--- a/solution.py
+++ b/solution.py
@@ -9,12 +9,21 @@
 
 BF16, F32 = jnp.bfloat16, jnp.float32
 MESH = pl.DeviceIdType.MESH
-AHEAD = 3
-
-
-def stack_kernel(n_sp, signal, cond, w_now, w_past, w_cond, b_gate, w_res, w_skip, h_out, skip_out,
-                 u, c, bias, w_in, w_mix, h, skip,
-                 sig_sem, cond_sem, bias_sem, w_sem, send_sem, recv_sem, out_sem):
+AHEAD = 2
+PIECES = 8
+
+
+def at_step(i, order):
+    code = i + (order[-1] - (len(order) - 1))
+    for j in range(len(order) - 2, -1, -1):
+        if order[j] - j != order[j + 1] - (j + 1):
+            code = jnp.where(i <= j, i + (order[j] - j), code)
+    return code
+
+
+def stack_kernel(n_sp, signal, cond, w_now, w_past, w_cond, b_gate, w_res, w_skip, h, skip,
+                 u, acts, c, bias, w_in, w_mix, w_sum,
+                 sig_sem, cond_sem, bias_sem, w_sem, send_sem, recv_sem, far_send_sem, far_recv_sem):
     batch, layers, two_span, ch = u.shape
     span = two_span // 2
     cond_ch = c.shape[2]
@@ -25,8 +34,8 @@
             (w_now.at[layer], w_in.at[layer, pl.ds(0, ch)]),
             (w_cond.at[layer], w_in.at[layer, pl.ds(ch, cond_ch)]),
             (w_past.at[layer], w_in.at[layer, pl.ds(ch + cond_ch, ch)]),
-            (w_res.at[layer], w_mix.at[layer, :, pl.ds(0, ch)]),
-            (w_skip.at[layer], w_mix.at[layer, :, pl.ds(ch, skip.shape[2])]),
+            (w_res.at[layer], w_mix.at[layer]),
+            (w_skip.at[layer], w_sum.at[pl.ds(layer * ch, ch)]),
         )
         return [pltpu.make_async_copy(src, dst, w_sem.at[layer, i]) for i, (src, dst) in enumerate(pairs)]
 
@@ -48,6 +57,14 @@
         @pl.when(me + hops(layer) < n_sp)
         def _():
             edge_copy(s, layer).start()
+
+    def far_copy(s, piece):
+        rows = span // PIECES
+        return pltpu.make_async_remote_copy(
+            src_ref=u.at[s, layers - 1, pl.ds(span + piece * rows, rows)],
+            dst_ref=u.at[s, layers - 1, pl.ds(piece * rows, rows)],
+            send_sem=far_send_sem.at[s, piece], recv_sem=far_recv_sem.at[s, piece],
+            device_id=(dp, lax.rem(me + hops(layers - 1), n_sp)), device_id_type=MESH)
 
     sig_in = [pltpu.make_async_copy(signal.at[s], u.at[s, 0, pl.ds(span, span)], sig_sem.at[s]) for s in range(batch)]
     cond_in = [pltpu.make_async_copy(cond.at[s], c.at[s], cond_sem.at[s]) for s in range(batch)]
@@ -95,7 +112,11 @@
 
         @pl.when(me >= hops(layer))
         def _():
-            edge_copy(s, layer).wait_recv()
+            if layer == layers - 1:
+                for piece in range(PIECES):
+                    far_copy(s, piece).wait_recv()
+            else:
+                edge_copy(s, layer).wait_recv()
 
         now = u[s, layer, span:]
         if dilation < 16:
@@ -113,39 +134,65 @@
             gated.append((jnp.tanh(zf) * (0.5 * jnp.tanh(0.5 * zg) + 0.5)).astype(BF16))
         a = jnp.concatenate(gated, axis=1)
         base = now.astype(F32) if layer == 0 else h[s]
-        new_h = base + jnp.dot(a, w_mix[layer, :, :ch], preferred_element_type=F32)
+        new_h = base + jnp.dot(a, w_mix[layer], preferred_element_type=F32)
         h[s] = new_h
         if layer + 1 < layers:
             u[s, layer + 1, span:] = new_h.astype(BF16)
-        new_skip = jnp.dot(a, w_mix[layer, :, ch:], preferred_element_type=F32)
-        skip[s] = new_skip if layer == 0 else skip[s] + new_skip
-        if layer + 1 < layers:
+            acts[s, :, layer * ch:(layer + 1) * ch] = a
+        else:
+            skip[s] += jnp.dot(a, w_sum[layer * ch:], preferred_element_type=F32)
+        if layer + 2 < layers:
             send_edge(s, layer + 1)
-        else:
-            pltpu.make_async_copy(h.at[s], h_out.at[s], out_sem.at[s, 0]).start()
-            pltpu.make_async_copy(skip.at[s], skip_out.at[s], out_sem.at[s, 1]).start()
+
+            @pl.when((s == 1) & (me + hops(layers - 1) < n_sp))
+            def _():
+                far_copy(0, layer).start()
+        elif layer + 1 < layers:
+            @pl.when((s == 1) & (me + hops(layers - 1) < n_sp))
+            def _():
+                for piece in range(PIECES):
+                    far_copy(1, piece).start()
+
+    def sum_skip(s):
+        skip[s] = jnp.dot(acts[s], w_sum[:(layers - 1) * ch], preferred_element_type=F32)
+
+    lead = [2 * k for k in range(9)]
+    early = lead + [2 * k + 1 for k in range(9)] + [20, 21, 18, 19]
+    late = lead[:8] + [1, 16] + [2 * k + 1 for k in range(1, 8)] + [20, 18, 17, 21, 19]
 
     def run(i, carry):
-        early = jnp.where(i < 9, i, jnp.where(i < 18, i + 1, jnp.where(i < 19, 9, 19)))
-        late = jnp.where(i < 8, i, jnp.where(i < 10, i + 2, jnp.where(i < 11, 8, jnp.where(
-            i < 17, i + 1, jnp.where(i < 18, 9, i)))))
-        code = jnp.where(me < n_sp // 2, early, late)
-        s, which = code // layers, code % layers
+        code = jnp.where(me < n_sp // 2, at_step(i, early), at_step(i, late))
+        s, which = code % batch, code // batch
         for layer in range(layers):
             @pl.when(which == layer)
             def _():
                 step(s, layer)
+
+        @pl.when(which == layers)
+        def _():
+            sum_skip(s)
         return carry
 
-    lax.fori_loop(0, batch * layers, run, 0)
+    lax.fori_loop(0, len(early), run, 0)
 
     for s in range(batch):
-        pltpu.make_async_copy(h.at[s], h_out.at[s], out_sem.at[s, 0]).wait()
-        pltpu.make_async_copy(skip.at[s], skip_out.at[s], out_sem.at[s, 1]).wait()
-        for layer in range(layers):
+        for layer in range(layers - 1):
             @pl.when(me + hops(layer) < n_sp)
             def _():
                 edge_copy(s, layer).wait_send()
+
+        @pl.when(me + hops(layers - 1) < n_sp)
+        def _():
+            for piece in range(PIECES):
+                far_copy(s, piece).wait_send()
+
+
+def store_kernel(h, skip, h_out, skip_out, sem):
+    copies = [pltpu.make_async_copy(h, h_out, sem.at[0]), pltpu.make_async_copy(skip, skip_out, sem.at[1])]
+    for copy in copies:
+        copy.start()
+    for copy in copies:
+        copy.wait()
 
 
 def solution(mesh):
@@ -155,29 +202,39 @@
         batch, span, ch = signal.shape
         layers, cond_ch, skip_ch = w_now.shape[0], cond_feats.shape[2], w_skip.shape[2]
         anywhere = pl.BlockSpec(memory_space=pl.ANY)
-        return pl.pallas_call(
+        in_vmem = pl.BlockSpec(memory_space=pltpu.VMEM)
+        h, skip = pl.pallas_call(
             functools.partial(stack_kernel, n_sp),
-            out_shape=[jax.ShapeDtypeStruct((batch, span, ch), F32), jax.ShapeDtypeStruct((batch, span, skip_ch), F32)],
-            in_specs=[anywhere] * 8,
-            out_specs=[anywhere] * 2,
+            out_shape=[pltpu.VMEM((batch, span, ch), F32), pltpu.VMEM((batch, span, skip_ch), F32)],
+            in_specs=[pl.BlockSpec(memory_space=pltpu.HBM)] * 8,
+            out_specs=[in_vmem] * 2,
             scratch_shapes=[
                 pltpu.VMEM((batch, layers, 2 * span, ch), BF16),
+                pltpu.VMEM((batch, span, (layers - 1) * ch), BF16),
                 pltpu.VMEM((batch, span, cond_ch), BF16),
                 pltpu.VMEM((layers, 2 * ch), F32),
                 pltpu.VMEM((layers, 2 * ch + cond_ch, 2 * ch), BF16),
-                pltpu.VMEM((layers, ch, ch + skip_ch), BF16),
-                pltpu.VMEM((batch, span, ch), F32),
-                pltpu.VMEM((batch, span, skip_ch), F32),
+                pltpu.VMEM((layers, ch, ch), BF16),
+                pltpu.VMEM((layers * ch, skip_ch), BF16),
                 pltpu.SemaphoreType.DMA((batch,)),
                 pltpu.SemaphoreType.DMA((batch,)),
                 pltpu.SemaphoreType.DMA,
                 pltpu.SemaphoreType.DMA((layers, 5)),
-                pltpu.SemaphoreType.DMA((batch, layers)),
-                pltpu.SemaphoreType.DMA((batch, layers)),
-                pltpu.SemaphoreType.DMA((batch, 2)),
+                pltpu.SemaphoreType.DMA((batch, layers - 1)),
+                pltpu.SemaphoreType.DMA((batch, layers - 1)),
+                pltpu.SemaphoreType.DMA((batch, PIECES)),
+                pltpu.SemaphoreType.DMA((batch, PIECES)),
             ],
             compiler_params=pltpu.CompilerParams(collective_id=0, has_side_effects=True, vmem_limit_bytes=60 * 2 ** 20),
         )(signal, cond_feats, w_now, w_past, w_cond, b_gate, w_res, w_skip)
+        return pl.pallas_call(
+            store_kernel,
+            out_shape=[jax.ShapeDtypeStruct((batch, span, ch), F32), jax.ShapeDtypeStruct((batch, span, skip_ch), F32)],
+            in_specs=[in_vmem] * 2,
+            out_specs=[anywhere] * 2,
+            scratch_shapes=[pltpu.SemaphoreType.DMA((2,))],
+            compiler_params=pltpu.CompilerParams(vmem_limit_bytes=2 ** 20),
+        )(h, skip)
 
     seq_spec = P('dp', 'sp', None)
     return jax.shard_map(local_stack, mesh=mesh,

time: 47.5 us -> 39.4 us (0.83)
  local copies, waits for them, and re-layouts: 4.13 us -> 0 us
  Pallas kernels: 42.6 us -> 38.7 us
    unnamed x2 -> x0, local copies, waits for them, and re-layouts: 4.13 us -> none
    pallas_call x1 -> x2, Pallas kernels: 42.6 us -> 38.7 us  [the longest x1 37.5 us: local_stack(): pl.pallas_call(functools.partial(stack_kernel, n_sp), out_shape=[pltpu.VM...]
where the time goes in v2:
time: 39.4 us; the launch traced here: 39.3 us
  Pallas kernels  38.7 us (98%)
  between operations  0.64 us (2%)
    pallas_call x1, Pallas kernels, local_stack(): pl.pallas_call(functools.partial(stack_kernel, n_sp), out_shape=[pltpu.VM...  37.5 us
    pallas_call x1, Pallas kernels, local_stack(): pl.pallas_call(store_kernel, out_shape=[jax.ShapeDtypeStruct((batch, span...  1.16 us

profile of v2, /device:TPU:7, one launch (start us, length us, event | category | flops | bytes accessed | tf_op | source)
XLA Modules:
  0.0 39.3 jit_solution(18135190798464159087)
XLA Ops:
  0.6 37.5 %shard_map.95 = (f32[2,256,512]{2,1,0:T(8,128)S(1)}, f32[2,256,256]{2,1,0:T(8,128)S(1)}) custom-call(bf16[2,256,512]{2,1,0:T(8,128)(2,1)} %signal.1, bf16[2,256,256]{2,1,0:T(8,128)(2,1)} %cond.1, bf16[10,512,1024]{2,1,0:T(8,128)(2,1)} %w_now.1, bf16[10,512,1024]{2,1,0:T(8,128)(2,1)} %w_past.1, bf16[10,256,1024]{2,1,0:T(8,128)(2,1)} %w_cond.1, ...), custom_call_target="tpu_custom_call" | custom-call | tf_op jit(solution)/shard_map/pallas_call | solution.py:206
  38.2 1.2 %shard_map.96 = (f32[2,256,512]{2,1,0:T(8,128)}, f32[2,256,256]{2,1,0:T(8,128)}) custom-call(f32[2,256,512]{2,1,0:T(8,128)S(1)} %get-tuple-element.4.h, f32[2,256,256]{2,1,0:T(8,128)S(1)} %get-tuple-element.5.skip), custom_call_target="tpu_custom_call" | custom-call | tf_op jit(solution)/shard_map/pallas_call | solution.py:230

commit v3 on v0

v3 whole, which is shorter than its diff:
```python
import functools

import jax
import jax.numpy as jnp
from jax import lax
from jax.experimental import pallas as pl
from jax.experimental.pallas import tpu as pltpu
from jax.sharding import PartitionSpec as P

BF16, F32 = jnp.bfloat16, jnp.float32
MESH = pl.DeviceIdType.MESH
TILE = 16
AHEAD = 2
PIECES = 8


def at_step(i, order):
    code = 2 * i + (order[-1] - 2 * (len(order) - 1))
    for j in range(len(order) - 2, -1, -1):
        if order[j] - 2 * j != order[j + 1] - 2 * (j + 1):
            code = jnp.where(i <= j, 2 * i + (order[j] - 2 * j), code)
    return code


def stack_kernel(n_sp, signal, cond, w_now, w_past, w_cond, b_gate, w_res, w_skip, h, skip,
                 u, acts, z_part, c, bias, w_in, w_mix, w_sum,
                 sig_sem, cond_sem, bias_sem, w_sem, sum_sem, send_sem, recv_sem, far_send_sem, far_recv_sem):
    batch, layers, span, ch = u.shape[0], w_in.shape[0], h.shape[1], h.shape[2]
    last, cond_ch = layers - 1, c.shape[2]
    dp, me = lax.axis_index('dp'), lax.axis_index('sp')

    sizes = [min(max(TILE, 2 ** k), span) for k in range(last)]
    groups = [(sizes.index(rows), len(sizes) - sizes[::-1].index(rows), rows) for rows in sorted(set(sizes))]
    far_hops = 2 ** last // span

    def start_weights(layer):
        slot = lax.rem(layer, AHEAD + 1)
        for src, dst in ((w_now.at[layer], w_in.at[layer, pl.ds(0, ch)]),
                         (w_cond.at[layer], w_in.at[layer, pl.ds(ch, cond_ch)]),
                         (w_past.at[layer], w_in.at[layer, pl.ds(ch + cond_ch, ch)])):
            pltpu.make_async_copy(src, dst, w_sem.at[slot, 0]).start()
        pltpu.make_async_copy(w_res.at[layer], w_mix.at[layer], w_sem.at[slot, 1]).start()

    def landed(ref, sem):
        pltpu.make_async_copy(ref, ref, sem).wait()

    def await_weights(layer):
        slot = lax.rem(layer, AHEAD + 1)
        landed(w_in.at[layer], w_sem.at[slot, 0])
        landed(w_mix.at[layer], w_sem.at[slot, 1])

    def edge_copy(s, layer, rows):
        return pltpu.make_async_remote_copy(
            src_ref=u.at[s, layer, pl.ds(2 * span - rows, rows)],
            dst_ref=u.at[s, layer, pl.ds(span - rows, rows)],
            send_sem=send_sem.at[s], recv_sem=recv_sem.at[s, layer],
            device_id=(dp, lax.rem(me + 1, n_sp)), device_id_type=MESH)

    def send_edge(s, layer):
        for first, end, rows in groups:
            @pl.when((layer >= first) & (layer < end) & (me + 1 < n_sp))
            def _():
                edge_copy(s, layer, rows).start()

    def far_copy(s, piece):
        rows = span // PIECES
        return pltpu.make_async_remote_copy(
            src_ref=u.at[s, last, pl.ds(span + piece * rows, rows)],
            dst_ref=u.at[s, last, pl.ds(piece * rows, rows)],
            send_sem=far_send_sem.at[s], recv_sem=far_recv_sem.at[s, piece // (PIECES // 2)],
            device_id=(dp, lax.rem(me + far_hops, n_sp)), device_id_type=MESH)

    sends_far = me + far_hops < n_sp

    sig_in = pltpu.make_async_copy(signal, u.at[:, 0, pl.ds(span, span)], sig_sem)
    cond_in = pltpu.make_async_copy(cond, c, cond_sem)
    bias_in = pltpu.make_async_copy(b_gate, bias, bias_sem)
    for copy in (sig_in, cond_in, bias_in):
        copy.start()
    for layer in range(AHEAD):
        start_weights(layer)

    barrier = pltpu.get_barrier_semaphore()
    for off in range(1, n_sp):
        pl.semaphore_signal(barrier, inc=1, device_id=(dp, lax.rem(me + off, n_sp)), device_id_type=MESH)

    @pl.when(me < 1)
    def _():
        for s in range(batch):
            for layer in range(last):
                u[s, layer, span - sizes[layer]:span] = jnp.zeros((sizes[layer], ch), BF16)

    @pl.when(me < far_hops)
    def _():
        for s in range(batch):
            u[s, last, :span] = jnp.zeros((span, ch), BF16)

    sig_in.wait()
    pl.semaphore_wait(barrier, n_sp - 1)
    for s in range(batch):
        send_edge(s, 0)
    for s in range(batch):
        h[s] = u[s, 0, span:].astype(F32)
    cond_in.wait()
    bias_in.wait()

    def gate(z):
        half = ch // 2
        parts = []
        for lo in (0, half):
            zf, zg = z(lo, lo + half), z(ch + lo, ch + lo + half)
            parts.append((jnp.tanh(zf) * (0.5 * jnp.tanh(0.5 * zg) + 0.5)).astype(BF16))
        return jnp.concatenate(parts, axis=1)

    def step(s, layer):
        @pl.when(s == 0)
        def _():
            @pl.when(layer < layers - AHEAD)
            def _():
                start_weights(layer + AHEAD)
            await_weights(layer)

        @pl.when((s == 1) & (layer == 1))
        def _():
            for k in range(layers):
                pltpu.make_async_copy(w_skip.at[k], w_sum.at[k], sum_sem).start()

        for first, end, rows in groups:
            @pl.when((layer >= first) & (layer < end) & (me >= 1))
            def _():
                edge_copy(s, layer, rows).wait_recv()

        dilation = jnp.left_shift(1, layer)

        def layer_body(past):
            x = jnp.concatenate([u[s, layer, span:], c[s], past], axis=1)
            a = gate(lambda lo, hi: jnp.dot(x, w_in[layer, :, lo:hi], preferred_element_type=F32) + bias[pl.ds(layer, 1), lo:hi])
            acts[s, layer] = a
            new_h = h[s] + jnp.dot(a, w_mix[layer], preferred_element_type=F32)
            h[s] = new_h
            u[s, layer + 1, span:] = new_h.astype(BF16)

        @pl.when(dilation < TILE)
        def _():
            wide = u[s, layer, span - TILE:].astype(F32)
            layer_body(pltpu.roll(wide, dilation, axis=0)[TILE:].astype(BF16))

        @pl.when(dilation >= TILE)
        def _():
            base = pl.multiple_of(span - jnp.minimum(dilation, span), TILE)
            layer_body(u[s, layer, pl.ds(base, span)])

        send_edge(s, layer + 1)

        @pl.when(sends_far)
        def _():
            @pl.when((s == 0) & (layer == last - 1))
            def _():
                far_copy(0, 0).start()

            @pl.when((s == 1) & (layer == 0))
            def _():
                for piece in range(1, PIECES - 5):
                    far_copy(0, piece).start()

            @pl.when((s == 1) & (layer >= 1) & (layer < 6))
            def _():
                far_copy(0, layer + PIECES - 6).start()

            @pl.when((s == 1) & (layer == last - 1))
            def _():
                for piece in range(PIECES):
                    far_copy(1, piece).start()

    def last_step(s):
        @pl.when(s == 0)
        def _():
            await_weights(last)

        near = jnp.concatenate([u[s, last, span:], c[s]], axis=1)
        depth = near.shape[1]
        z_part[...] = jnp.dot(near, w_in[last, :depth], preferred_element_type=F32) + bias[last:, :]

        rows = span // 2

        def finish(part, carry):
            at = pl.ds(pl.multiple_of(part * rows, rows), rows)

            @pl.when(me >= far_hops)
            def _():
                landed(u.at[s, last, at], far_recv_sem.at[s, part])

            past = u[s, last, at]
            a = gate(lambda lo, hi: z_part[at, lo:hi] + jnp.dot(past, w_in[last, depth:, lo:hi], preferred_element_type=F32))
            h[s, at] += jnp.dot(a, w_mix[last], preferred_element_type=F32)
            skip[s, at] += jnp.dot(a, w_sum[last], preferred_element_type=F32)
            return carry

        lax.fori_loop(0, 2, finish, 0)

    def sum_skip(s):
        @pl.when(s == 0)
        def _():
            landed(w_sum, sum_sem)

        x = jnp.concatenate([acts[s, k] for k in range(last)], axis=1)
        skip[s] = jnp.dot(x, w_sum[:last].reshape(last * ch, skip.shape[2]), preferred_element_type=F32)

    early = [2 * k for k in range(9)] + [2 * k + 1 for k in range(9)] + [20, 21, 18, 19]
    late = [0, 1] + [2 * k for k in range(1, 9)] + [2 * k + 1 for k in range(1, 8)] + [20, 18, 17, 21, 19]

    def run(i, carry):
        code = jnp.where(me < n_sp // 2, at_step(i, early), at_step(i, late))
        s, layer = code % batch, code // batch

        @pl.when(layer < last)
        def _():
            step(s, layer)

        @pl.when(layer == last)
        def _():
            last_step(s)

        @pl.when(layer == layers)
        def _():
            sum_skip(s)
        return carry

    lax.fori_loop(0, len(early), run, 0)

    parts = next(n for n in range(1, layers) if sum(sizes) % (n * TILE) == 0 and sum(sizes) <= n * span)
    for s in range(batch):
        @pl.when(me + 1 < n_sp)
        def _():
            landed(u.at[s, pl.ds(0, parts), pl.ds(0, sum(sizes) // parts)], send_sem.at[s])

        @pl.when(sends_far)
        def _():
            landed(u.at[s, last, pl.ds(0, span)], far_send_sem.at[s])


def store_kernel(h, skip, h_out, skip_out, sem):
    copies = [pltpu.make_async_copy(h, h_out, sem.at[0]), pltpu.make_async_copy(skip, skip_out, sem.at[1])]
    for copy in copies:
        copy.start()
    for copy in copies:
        copy.wait()


def solution(mesh):
    n_sp = mesh.shape['sp']

    def local_stack(signal, cond_feats, w_now, w_past, w_cond, b_gate, w_res, w_skip):
        batch, span, ch = signal.shape
        layers, cond_ch, skip_ch = w_now.shape[0], cond_feats.shape[2], w_skip.shape[2]
        in_vmem = pl.BlockSpec(memory_space=pltpu.VMEM)
        h, skip = pl.pallas_call(
            functools.partial(stack_kernel, n_sp),
            out_shape=[pltpu.VMEM((batch, span, ch), F32), pltpu.VMEM((batch, span, skip_ch), F32)],
            in_specs=[pl.BlockSpec(memory_space=pltpu.HBM)] * 8,
            out_specs=[in_vmem] * 2,
            scratch_shapes=[
                pltpu.VMEM((batch, layers, 2 * span, ch), BF16),
                pltpu.VMEM((batch, layers - 1, span, ch), BF16),
                pltpu.VMEM((span, 2 * ch), F32),
                pltpu.VMEM((batch, span, cond_ch), BF16),
                pltpu.VMEM((layers, 2 * ch), F32),
                pltpu.VMEM((layers, 2 * ch + cond_ch, 2 * ch), BF16),
                pltpu.VMEM((layers, ch, ch), BF16),
                pltpu.VMEM((layers, ch, skip_ch), BF16),
                pltpu.SemaphoreType.DMA,
                pltpu.SemaphoreType.DMA,
                pltpu.SemaphoreType.DMA,
                pltpu.SemaphoreType.DMA((AHEAD + 1, 2)),
                pltpu.SemaphoreType.DMA,
                pltpu.SemaphoreType.DMA((batch,)),
                pltpu.SemaphoreType.DMA((batch, layers - 1)),
                pltpu.SemaphoreType.DMA((batch,)),
                pltpu.SemaphoreType.DMA((batch, 2)),
            ],
            compiler_params=pltpu.CompilerParams(collective_id=0, has_side_effects=True, vmem_limit_bytes=60 * 2 ** 20),
        )(signal, cond_feats, w_now, w_past, w_cond, b_gate, w_res, w_skip)
        return pl.pallas_call(
            store_kernel,
            out_shape=[jax.ShapeDtypeStruct((batch, span, ch), F32), jax.ShapeDtypeStruct((batch, span, skip_ch), F32)],
            in_specs=[in_vmem] * 2,
            out_specs=[pl.BlockSpec(memory_space=pl.ANY)] * 2,
            scratch_shapes=[pltpu.SemaphoreType.DMA((2,))],
            compiler_params=pltpu.CompilerParams(vmem_limit_bytes=2 ** 20),
        )(h, skip)

    seq_spec = P('dp', 'sp', None)
    return jax.shard_map(local_stack, mesh=mesh,
                         in_specs=(seq_spec, seq_spec, P(), P(), P(), P(), P(), P()),
                         out_specs=(seq_spec, seq_spec), check_vma=False)
```

time: 107 us -> 38 us (0.36)
  the two profiles are of different devices: /device:TPU:0 before, /device:TPU:7 now
where the time goes in v3:
time: 38 us; the launch traced here: 37.9 us
  Pallas kernels  37.3 us (98%)
  between operations  0.64 us (2%)
    pallas_call x1, Pallas kernels, local_stack(): pl.pallas_call(functools.partial(stack_kernel, n_sp), out_shape=[pltpu.VM...  36.1 us
    pallas_call x1, Pallas kernels, local_stack(): pl.pallas_call(store_kernel, out_shape=[jax.ShapeDtypeStruct((batch, span...  1.16 us

profile of v3, /device:TPU:7, one launch (start us, length us, event | category | flops | bytes accessed | tf_op | source)
XLA Modules:
  0.0 37.9 jit_solution(7861400286097987799)
XLA Ops:
  0.6 36.1 %shard_map.95 = (f32[2,256,512]{2,1,0:T(8,128)S(1)}, f32[2,256,256]{2,1,0:T(8,128)S(1)}) custom-call(bf16[2,256,512]{2,1,0:T(8,128)(2,1)} %signal.1, bf16[2,256,256]{2,1,0:T(8,128)(2,1)} %cond.1, bf16[10,512,1024]{2,1,0:T(8,128)(2,1)} %w_now.1, bf16[10,512,1024]{2,1,0:T(8,128)(2,1)} %w_past.1, bf16[10,256,1024]{2,1,0:T(8,128)(2,1)} %w_cond.1, ...), custom_call_target="tpu_custom_call" | custom-call | tf_op jit(solution)/shard_map/pallas_call | solution.py:257
  36.7 1.2 %shard_map.96 = (f32[2,256,512]{2,1,0:T(8,128)}, f32[2,256,256]{2,1,0:T(8,128)}) custom-call(f32[2,256,512]{2,1,0:T(8,128)S(1)} %get-tuple-element.4.h, f32[2,256,256]{2,1,0:T(8,128)S(1)} %get-tuple-element.5.skip), custom_call_target="tpu_custom_call" | custom-call | tf_op jit(solution)/shard_map/pallas_call | solution.py:283

commit v4 on v3

--- a/solution.py
+++ b/solution.py
@@ -22,15 +22,16 @@
     return code
 
 
-def stack_kernel(n_sp, signal, cond, w_now, w_past, w_cond, b_gate, w_res, w_skip, h, skip,
-                 u, acts, z_part, c, bias, w_in, w_mix, w_sum,
-                 sig_sem, cond_sem, bias_sem, w_sem, sum_sem, send_sem, recv_sem, far_send_sem, far_recv_sem):
-    batch, layers, span, ch = u.shape[0], w_in.shape[0], h.shape[1], h.shape[2]
+def stack_kernel(n_sp, signal, cond, w_now, w_past, w_cond, b_gate, w_res, w_skip, h_out, skip,
+                 u, h, acts, z_part, c, bias, w_in, w_mix, w_sum,
+                 sig_sem, cond_sem, bias_sem, w_sem, sum_sem, send_sem, recv_sem, far_send_sem, far_recv_sem,
+                 cond_send_sem, cond_recv_sem):
+    batch, layers, span, ch = u.shape[0], w_in.shape[0], h_out.shape[1], h_out.shape[2]
     last, cond_ch = layers - 1, c.shape[2]
     dp, me = lax.axis_index('dp'), lax.axis_index('sp')
 
-    sizes = [min(max(TILE, 2 ** k), span) for k in range(last)]
-    groups = [(sizes.index(rows), len(sizes) - sizes[::-1].index(rows), rows) for rows in sorted(set(sizes))]
+    near = next(k for k in range(layers) if 2 ** k >= TILE)
+    sizes = {k: min(max(TILE, 2 ** k), span) for k in range(last) if k == 0 or k >= near}
     far_hops = 2 ** last // span
 
     def start_weights(layer):
@@ -57,10 +58,16 @@
             device_id=(dp, lax.rem(me + 1, n_sp)), device_id_type=MESH)
 
     def send_edge(s, layer):
-        for first, end, rows in groups:
-            @pl.when((layer >= first) & (layer < end) & (me + 1 < n_sp))
-            def _():
-                edge_copy(s, layer, rows).start()
+        for k, rows in sizes.items():
+            @pl.when((layer == k) & (me + 1 < n_sp))
+            def _():
+                edge_copy(s, k, rows).start()
+
+    def cond_copy(s):
+        return pltpu.make_async_remote_copy(
+            src_ref=c.at[s, pl.ds(span, TILE)], dst_ref=c.at[s, pl.ds(0, TILE)],
+            send_sem=cond_send_sem, recv_sem=cond_recv_sem.at[s],
+            device_id=(dp, lax.rem(me + 1, n_sp)), device_id_type=MESH)
 
     def far_copy(s, piece):
         rows = span // PIECES
@@ -73,35 +80,63 @@
     sends_far = me + far_hops < n_sp
 
     sig_in = pltpu.make_async_copy(signal, u.at[:, 0, pl.ds(span, span)], sig_sem)
-    cond_in = pltpu.make_async_copy(cond, c, cond_sem)
+    cond_in = pltpu.make_async_copy(cond, c.at[:, pl.ds(TILE, span)], cond_sem)
     bias_in = pltpu.make_async_copy(b_gate, bias, bias_sem)
     for copy in (sig_in, cond_in, bias_in):
         copy.start()
-    for layer in range(AHEAD):
-        start_weights(layer)
+    start_weights(0)
 
     barrier = pltpu.get_barrier_semaphore()
-    for off in range(1, n_sp):
-        pl.semaphore_signal(barrier, inc=1, device_id=(dp, lax.rem(me + off, n_sp)), device_id_type=MESH)
+    chip = n_sp // 2
+    partner = me + 1 - 2 * lax.rem(me, 2)
+    pl.semaphore_signal(barrier, inc=1, device_id=(dp, partner), device_id_type=MESH)
+
+    def greet_other_chip():
+        for core in range(chip):
+            pl.semaphore_signal(barrier, inc=1, device_id=(dp, (1 - me // chip) * chip + core), device_id_type=MESH)
 
     @pl.when(me < 1)
     def _():
         for s in range(batch):
-            for layer in range(last):
-                u[s, layer, span - sizes[layer]:span] = jnp.zeros((sizes[layer], ch), BF16)
+            for layer, rows in sizes.items():
+                u[s, layer, span - rows:span] = jnp.zeros((rows, ch), BF16)
 
     @pl.when(me < far_hops)
     def _():
         for s in range(batch):
             u[s, last, :span] = jnp.zeros((span, ch), BF16)
 
+    @pl.when(me < chip)
+    def _():
+        pl.semaphore_wait(barrier, 1)
+        greet_other_chip()
+
+    @pl.when(me >= chip)
+    def _():
+        pl.semaphore_wait(barrier, n_sp - 1)
+        greet_other_chip()
+
     sig_in.wait()
-    pl.semaphore_wait(barrier, n_sp - 1)
+    for layer in range(1, AHEAD):
+        start_weights(layer)
+    cond_in.wait()
+
+    def send_first():
+        for s in range(batch):
+            edge_copy(s, 0, sizes[0]).start()
+            cond_copy(s).start()
+
+    @pl.when(me == chip - 1)
+    def _():
+        pl.semaphore_wait(barrier, chip)
+
+    @pl.when(me + 1 < n_sp)
+    def _():
+        send_first()
+
     for s in range(batch):
-        send_edge(s, 0)
-    for s in range(batch):
-        h[s] = u[s, 0, span:].astype(F32)
-    cond_in.wait()
+        h[s, TILE:] = u[s, 0, span:].astype(F32)
+        h[s, :TILE] = jnp.zeros((TILE, ch), F32)
     bias_in.wait()
 
     def gate(z):
@@ -115,40 +150,54 @@
     def step(s, layer):
         @pl.when(s == 0)
         def _():
+            await_weights(layer)
+
             @pl.when(layer < layers - AHEAD)
             def _():
                 start_weights(layer + AHEAD)
-            await_weights(layer)
-
-        @pl.when((s == 1) & (layer == 1))
+
+        @pl.when((s == 0) & (layer == last - 2))
         def _():
             for k in range(layers):
                 pltpu.make_async_copy(w_skip.at[k], w_sum.at[k], sum_sem).start()
 
-        for first, end, rows in groups:
-            @pl.when((layer >= first) & (layer < end) & (me >= 1))
-            def _():
-                edge_copy(s, layer, rows).wait_recv()
+        for k, rows in sizes.items():
+            @pl.when((layer == k) & (me >= 1))
+            def _():
+                edge_copy(s, k, rows).wait_recv()
+                if k == 0:
+                    cond_copy(s).wait_recv()
+                    h[s, :TILE] = u[s, 0, span - TILE:span].astype(F32)
 
         dilation = jnp.left_shift(1, layer)
 
-        def layer_body(past):
-            x = jnp.concatenate([u[s, layer, span:], c[s], past], axis=1)
+        def layer_body(ahead, past):
+            x = jnp.concatenate([u[s, layer, span - ahead:], c[s, TILE - ahead:], past], axis=1)
             a = gate(lambda lo, hi: jnp.dot(x, w_in[layer, :, lo:hi], preferred_element_type=F32) + bias[pl.ds(layer, 1), lo:hi])
-            acts[s, layer] = a
-            new_h = h[s] + jnp.dot(a, w_mix[layer], preferred_element_type=F32)
-            h[s] = new_h
-            u[s, layer + 1, span:] = new_h.astype(BF16)
-
-        @pl.when(dilation < TILE)
-        def _():
-            wide = u[s, layer, span - TILE:].astype(F32)
-            layer_body(pltpu.roll(wide, dilation, axis=0)[TILE:].astype(BF16))
-
-        @pl.when(dilation >= TILE)
+            acts[s, layer] = a[ahead:]
+            new_h = h[s, TILE - ahead:] + jnp.dot(a, w_mix[layer], preferred_element_type=F32)
+            h[s, TILE - ahead:] = new_h
+            new_u = new_h.astype(BF16)
+            u[s, layer + 1, span:] = new_u[ahead:]
+            return new_u[:ahead]
+
+        @pl.when(layer < near)
+        def _():
+            wide = u[s, layer, span - 2 * TILE:].astype(F32)
+            edge = layer_body(TILE, pltpu.roll(wide, dilation, axis=0)[TILE:].astype(BF16))
+
+            @pl.when(layer + 1 < near)
+            def _():
+                u[s, layer + 1, span - TILE:span] = jnp.where(me > 0, edge, jnp.zeros_like(edge))
+
+        @pl.when(layer >= near)
         def _():
             base = pl.multiple_of(span - jnp.minimum(dilation, span), TILE)
-            layer_body(u[s, layer, pl.ds(base, span)])
+            layer_body(0, u[s, layer, pl.ds(base, span)])
+
+        @pl.when((s == 0) & (layer == 0) & (me < chip - 1))
+        def _():
+            pl.semaphore_wait(barrier, chip)
 
         send_edge(s, layer + 1)
 
@@ -177,9 +226,9 @@
         def _():
             await_weights(last)
 
-        near = jnp.concatenate([u[s, last, span:], c[s]], axis=1)
-        depth = near.shape[1]
-        z_part[...] = jnp.dot(near, w_in[last, :depth], preferred_element_type=F32) + bias[last:, :]
+        x = jnp.concatenate([u[s, last, span:], c[s, TILE:]], axis=1)
+        depth = x.shape[1]
+        z_part[...] = jnp.dot(x, w_in[last, :depth], preferred_element_type=F32) + bias[last:, :]
 
         rows = span // 2
 
@@ -192,7 +241,7 @@
 
             past = u[s, last, at]
             a = gate(lambda lo, hi: z_part[at, lo:hi] + jnp.dot(past, w_in[last, depth:, lo:hi], preferred_element_type=F32))
-            h[s, at] += jnp.dot(a, w_mix[last], preferred_element_type=F32)
+            h_out[s, at] = h[s, pl.ds(pl.multiple_of(TILE + part * rows, TILE), rows)] + jnp.dot(a, w_mix[last], preferred_element_type=F32)
             skip[s, at] += jnp.dot(a, w_sum[last], preferred_element_type=F32)
             return carry
 
@@ -207,7 +256,7 @@
         skip[s] = jnp.dot(x, w_sum[:last].reshape(last * ch, skip.shape[2]), preferred_element_type=F32)
 
     early = [2 * k for k in range(9)] + [2 * k + 1 for k in range(9)] + [20, 21, 18, 19]
-    late = [0, 1] + [2 * k for k in range(1, 9)] + [2 * k + 1 for k in range(1, 8)] + [20, 18, 17, 21, 19]
+    late = [0, 2, 4, 6, 1, 3, 5, 7] + [2 * k for k in range(4, 9)] + [20] + [2 * k + 1 for k in range(4, 8)] + [18, 17, 21, 19]
 
     def run(i, carry):
         code = jnp.where(me < n_sp // 2, at_step(i, early), at_step(i, late))
@@ -228,15 +277,20 @@
 
     lax.fori_loop(0, len(early), run, 0)
 
-    parts = next(n for n in range(1, layers) if sum(sizes) % (n * TILE) == 0 and sum(sizes) <= n * span)
+    total = sum(sizes.values())
+    parts = next(n for n in range(1, layers) if total % (n * TILE) == 0 and total <= n * 2 * span)
     for s in range(batch):
         @pl.when(me + 1 < n_sp)
         def _():
-            landed(u.at[s, pl.ds(0, parts), pl.ds(0, sum(sizes) // parts)], send_sem.at[s])
+            landed(u.at[s, pl.ds(0, parts), pl.ds(0, total // parts)], send_sem.at[s])
 
         @pl.when(sends_far)
         def _():
             landed(u.at[s, last, pl.ds(0, span)], far_send_sem.at[s])
+
+    @pl.when(me + 1 < n_sp)
+    def _():
+        landed(c.at[:, pl.ds(span, TILE)], cond_send_sem)
 
 
 def store_kernel(h, skip, h_out, skip_out, sem):
@@ -261,9 +315,10 @@
             out_specs=[in_vmem] * 2,
             scratch_shapes=[
                 pltpu.VMEM((batch, layers, 2 * span, ch), BF16),
+                pltpu.VMEM((batch, span + TILE, ch), F32),
                 pltpu.VMEM((batch, layers - 1, span, ch), BF16),
                 pltpu.VMEM((span, 2 * ch), F32),
-                pltpu.VMEM((batch, span, cond_ch), BF16),
+                pltpu.VMEM((batch, span + TILE, cond_ch), BF16),
                 pltpu.VMEM((layers, 2 * ch), F32),
                 pltpu.VMEM((layers, 2 * ch + cond_ch, 2 * ch), BF16),
                 pltpu.VMEM((layers, ch, ch), BF16),
@@ -277,6 +332,8 @@
                 pltpu.SemaphoreType.DMA((batch, layers - 1)),
                 pltpu.SemaphoreType.DMA((batch,)),
                 pltpu.SemaphoreType.DMA((batch, 2)),
+                pltpu.SemaphoreType.DMA,
+                pltpu.SemaphoreType.DMA((batch,)),
             ],
             compiler_params=pltpu.CompilerParams(collective_id=0, has_side_effects=True, vmem_limit_bytes=60 * 2 ** 20),
         )(signal, cond_feats, w_now, w_past, w_cond, b_gate, w_res, w_skip)

time: 38 us -> 37 us (0.974)
  Pallas kernels: 37.3 us -> 36.2 us
    pallas_call x1, Pallas kernels: 36.1 us -> 35.1 us  [local_stack(): pl.pallas_call(functools.partial(stack_kernel, n_sp), out_shape=[pltpu.VM...]
where the time goes in v4:
time: 37 us; the launch traced here: 36.9 us
  Pallas kernels  36.2 us (98%)
  between operations  0.64 us (2%)
    pallas_call x1, Pallas kernels, local_stack(): pl.pallas_call(functools.partial(stack_kernel, n_sp), out_shape=[pltpu.VM...  35.1 us
    pallas_call x1, Pallas kernels, local_stack(): pl.pallas_call(store_kernel, out_shape=[jax.ShapeDtypeStruct((batch, span...  1.16 us

profile of v4, /device:TPU:7, one launch (start us, length us, event | category | flops | bytes accessed | tf_op | source)
XLA Modules:
  0.0 36.9 jit_solution(5312650629422565574)
XLA Ops:
  0.6 35.1 %shard_map.95 = (f32[2,256,512]{2,1,0:T(8,128)S(1)}, f32[2,256,256]{2,1,0:T(8,128)S(1)}) custom-call(bf16[2,256,512]{2,1,0:T(8,128)(2,1)} %signal.1, bf16[2,256,256]{2,1,0:T(8,128)(2,1)} %cond.1, bf16[10,512,1024]{2,1,0:T(8,128)(2,1)} %w_now.1, bf16[10,512,1024]{2,1,0:T(8,128)(2,1)} %w_past.1, bf16[10,256,1024]{2,1,0:T(8,128)(2,1)} %w_cond.1, ...), custom_call_target="tpu_custom_call" | custom-call | tf_op jit(solution)/shard_map/pallas_call | solution.py:311
  35.7 1.2 %shard_map.96 = (f32[2,256,512]{2,1,0:T(8,128)}, f32[2,256,256]{2,1,0:T(8,128)}) custom-call(f32[2,256,512]{2,1,0:T(8,128)S(1)} %get-tuple-element.4.h, f32[2,256,256]{2,1,0:T(8,128)S(1)} %get-tuple-element.5.skip), custom_call_target="tpu_custom_call" | custom-call | tf_op jit(solution)/shard_map/pallas_call | solution.py:340

commit v5 on v4

--- a/solution.py
+++ b/solution.py
@@ -57,11 +57,15 @@
             send_sem=send_sem.at[s], recv_sem=recv_sem.at[s, layer],
             device_id=(dp, lax.rem(me + 1, n_sp)), device_id_type=MESH)
 
-    def send_edge(s, layer):
-        for k, rows in sizes.items():
-            @pl.when((layer == k) & (me + 1 < n_sp))
-            def _():
-                edge_copy(s, k, rows).start()
+    def pick(layer, layers, act):
+        if len(layers) == 1:
+            act(layers[0])
+            return
+        middle = len(layers) // 2
+        lax.cond(layer < layers[middle],
+                 lambda: pick(layer, layers[:middle], act), lambda: pick(layer, layers[middle:], act))
+
+    exchanged = list(range(near, last))
 
     def cond_copy(s):
         return pltpu.make_async_remote_copy(
@@ -156,18 +160,10 @@
             def _():
                 start_weights(layer + AHEAD)
 
-        @pl.when((s == 0) & (layer == last - 2))
-        def _():
-            for k in range(layers):
-                pltpu.make_async_copy(w_skip.at[k], w_sum.at[k], sum_sem).start()
-
-        for k, rows in sizes.items():
-            @pl.when((layer == k) & (me >= 1))
-            def _():
-                edge_copy(s, k, rows).wait_recv()
-                if k == 0:
-                    cond_copy(s).wait_recv()
-                    h[s, :TILE] = u[s, 0, span - TILE:span].astype(F32)
+            @pl.when(layer == last - 2)
+            def _():
+                for k in range(layers):
+                    pltpu.make_async_copy(w_skip.at[k], w_sum.at[k], sum_sem).start()
 
         dilation = jnp.left_shift(1, layer)
 
@@ -181,45 +177,61 @@
             u[s, layer + 1, span:] = new_u[ahead:]
             return new_u[:ahead]
 
-        @pl.when(layer < near)
-        def _():
+        def small():
+            @pl.when((layer == 0) & (me >= 1))
+            def _():
+                edge_copy(s, 0, sizes[0]).wait_recv()
+                cond_copy(s).wait_recv()
+                h[s, :TILE] = u[s, 0, span - TILE:span].astype(F32)
+
             wide = u[s, layer, span - 2 * TILE:].astype(F32)
             edge = layer_body(TILE, pltpu.roll(wide, dilation, axis=0)[TILE:].astype(BF16))
 
-            @pl.when(layer + 1 < near)
-            def _():
+            def keep_edge():
                 u[s, layer + 1, span - TILE:span] = jnp.where(me > 0, edge, jnp.zeros_like(edge))
 
-        @pl.when(layer >= near)
-        def _():
+            def send():
+                @pl.when(me + 1 < n_sp)
+                def _():
+                    edge_copy(s, near, sizes[near]).start()
+
+            lax.cond(layer + 1 < near, keep_edge, send)
+
+            @pl.when((layer == 0) & (s == 0) & (me < chip - 1))
+            def _():
+                pl.semaphore_wait(barrier, chip)
+
+        def large():
+            @pl.when(me >= 1)
+            def _():
+                pick(layer, exchanged, lambda k: edge_copy(s, k, sizes[k]).wait_recv())
+
             base = pl.multiple_of(span - jnp.minimum(dilation, span), TILE)
             layer_body(0, u[s, layer, pl.ds(base, span)])
 
-        @pl.when((s == 0) & (layer == 0) & (me < chip - 1))
-        def _():
-            pl.semaphore_wait(barrier, chip)
-
-        send_edge(s, layer + 1)
+            @pl.when((me + 1 < n_sp) & (layer + 1 < last))
+            def _():
+                pick(layer + 1, exchanged[1:], lambda k: edge_copy(s, k, sizes[k]).start())
+
+        lax.cond(layer < near, small, large)
 
         @pl.when(sends_far)
         def _():
-            @pl.when((s == 0) & (layer == last - 1))
-            def _():
-                far_copy(0, 0).start()
-
-            @pl.when((s == 1) & (layer == 0))
-            def _():
-                for piece in range(1, PIECES - 5):
-                    far_copy(0, piece).start()
-
-            @pl.when((s == 1) & (layer >= 1) & (layer < 6))
-            def _():
-                far_copy(0, layer + PIECES - 6).start()
-
-            @pl.when((s == 1) & (layer == last - 1))
-            def _():
-                for piece in range(PIECES):
-                    far_copy(1, piece).start()
+            def pieces(s, first, end):
+                for piece in range(first, end):
+                    far_copy(s, piece).start()
+
+            def first_sequence():
+                @pl.when(layer == last - 1)
+                def _():
+                    pieces(0, 0, 1)
+
+            def second_sequence():
+                pick(layer, list(range(last)), lambda k: (
+                    pieces(0, 1, 3) if k == 0 else pieces(0, k + 2, k + 3) if k < 6
+                    else pieces(1, 0, PIECES) if k == last - 1 else None))
+
+            lax.cond(s == 0, first_sequence, second_sequence)
 
     def last_step(s):
         @pl.when(s == 0)
@@ -262,17 +274,8 @@
         code = jnp.where(me < n_sp // 2, at_step(i, early), at_step(i, late))
         s, layer = code % batch, code // batch
 
-        @pl.when(layer < last)
-        def _():
-            step(s, layer)
-
-        @pl.when(layer == last)
-        def _():
-            last_step(s)
-
-        @pl.when(layer == layers)
-        def _():
-            sum_skip(s)
+        lax.cond(layer < last, lambda: step(s, layer),
+                 lambda: lax.cond(layer == last, lambda: last_step(s), lambda: sum_skip(s)))
         return carry
 
     lax.fori_loop(0, len(early), run, 0)

time: 37 us -> 37 us (level)
  no operation moved by 1% of the time
where the time goes in v5:
time: 37 us; the launch traced here: 36.7 us
  Pallas kernels  36 us (97%)
  between operations  0.64 us (2%)
    pallas_call x1, Pallas kernels, local_stack(): pl.pallas_call(functools.partial(stack_kernel, n_sp), out_shape=[pltpu.VM...  34.9 us
    pallas_call x1, Pallas kernels, local_stack(): pl.pallas_call(store_kernel, out_shape=[jax.ShapeDtypeStruct((batch, span...  1.16 us

profile of v5, /device:TPU:7, one launch (start us, length us, event | category | flops | bytes accessed | tf_op | source)
XLA Modules:
  0.0 36.7 jit_solution(7626645656418539680)
XLA Ops:
  0.6 34.9 %shard_map.95 = (f32[2,256,512]{2,1,0:T(8,128)S(1)}, f32[2,256,256]{2,1,0:T(8,128)S(1)}) custom-call(bf16[2,256,512]{2,1,0:T(8,128)(2,1)} %signal.1, bf16[2,256,256]{2,1,0:T(8,128)(2,1)} %cond.1, bf16[10,512,1024]{2,1,0:T(8,128)(2,1)} %w_now.1, bf16[10,512,1024]{2,1,0:T(8,128)(2,1)} %w_past.1, bf16[10,256,1024]{2,1,0:T(8,128)(2,1)} %w_cond.1, ...), custom_call_target="tpu_custom_call" | custom-call | tf_op jit(solution)/shard_map/pallas_call | solution.py:314
  35.5 1.2 %shard_map.96 = (f32[2,256,512]{2,1,0:T(8,128)}, f32[2,256,256]{2,1,0:T(8,128)}) custom-call(f32[2,256,512]{2,1,0:T(8,128)S(1)} %get-tuple-element.4.h, f32[2,256,256]{2,1,0:T(8,128)S(1)} %get-tuple-element.5.skip), custom_call_target="tpu_custom_call" | custom-call | tf_op jit(solution)/shard_map/pallas_call | solution.py:343

commit v6 on v5

--- a/solution.py
+++ b/solution.py
@@ -54,7 +54,7 @@
         return pltpu.make_async_remote_copy(
             src_ref=u.at[s, layer, pl.ds(2 * span - rows, rows)],
             dst_ref=u.at[s, layer, pl.ds(span - rows, rows)],
-            send_sem=send_sem.at[s], recv_sem=recv_sem.at[s, layer],
+            send_sem=send_sem.at[s], recv_sem=recv_sem.at[s, layer if layer < 1 else layer - near + 1],
             device_id=(dp, lax.rem(me + 1, n_sp)), device_id_type=MESH)
 
     def pick(layer, layers, act):
@@ -120,9 +120,9 @@
         pl.semaphore_wait(barrier, n_sp - 1)
         greet_other_chip()
 
-    sig_in.wait()
     for layer in range(1, AHEAD):
         start_weights(layer)
+    sig_in.wait()
     cond_in.wait()
 
     def send_first():
@@ -154,16 +154,11 @@
     def step(s, layer):
         @pl.when(s == 0)
         def _():
+            @pl.when(layer < layers - AHEAD)
+            def _():
+                start_weights(layer + AHEAD)
+
             await_weights(layer)
-
-            @pl.when(layer < layers - AHEAD)
-            def _():
-                start_weights(layer + AHEAD)
-
-            @pl.when(layer == last - 2)
-            def _():
-                for k in range(layers):
-                    pltpu.make_async_copy(w_skip.at[k], w_sum.at[k], sum_sem).start()
 
         dilation = jnp.left_shift(1, layer)
 
@@ -202,6 +197,11 @@
                 pl.semaphore_wait(barrier, chip)
 
         def large():
+            @pl.when((s == 1) & (layer == near))
+            def _():
+                for k in range(layers):
+                    pltpu.make_async_copy(w_skip.at[k], w_sum.at[k], sum_sem).start()
+
             @pl.when(me >= 1)
             def _():
                 pick(layer, exchanged, lambda k: edge_copy(s, k, sizes[k]).wait_recv())
@@ -268,7 +268,7 @@
         skip[s] = jnp.dot(x, w_sum[:last].reshape(last * ch, skip.shape[2]), preferred_element_type=F32)
 
     early = [2 * k for k in range(9)] + [2 * k + 1 for k in range(9)] + [20, 21, 18, 19]
-    late = [0, 2, 4, 6, 1, 3, 5, 7] + [2 * k for k in range(4, 9)] + [20] + [2 * k + 1 for k in range(4, 8)] + [18, 17, 21, 19]
+    late = [0, 2, 4, 6, 1, 3, 5, 7] + [2 * k for k in range(4, 9)] + [2 * k + 1 for k in range(4, 8)] + [20, 18, 17, 21, 19]
 
     def run(i, carry):
         code = jnp.where(me < n_sp // 2, at_step(i, early), at_step(i, late))
@@ -332,7 +332,7 @@
                 pltpu.SemaphoreType.DMA((AHEAD + 1, 2)),
                 pltpu.SemaphoreType.DMA,
                 pltpu.SemaphoreType.DMA((batch,)),
-                pltpu.SemaphoreType.DMA((batch, layers - 1)),
+                pltpu.SemaphoreType.DMA((batch, 6)),
                 pltpu.SemaphoreType.DMA((batch,)),
                 pltpu.SemaphoreType.DMA((batch, 2)),
                 pltpu.SemaphoreType.DMA,

time: 37 us -> 36.4 us (0.984)
  Pallas kernels: 36 us -> 35.5 us
    pallas_call x1, Pallas kernels: 34.9 us -> 34.3 us  [local_stack(): pl.pallas_call(functools.partial(stack_kernel, n_sp), out_shape=[pltpu.VM...]
where the time goes in v6:
time: 36.4 us; the launch traced here: 36.1 us
  Pallas kernels  35.5 us (98%)
  between operations  0.64 us (2%)
    pallas_call x1, Pallas kernels, local_stack(): pl.pallas_call(functools.partial(stack_kernel, n_sp), out_shape=[pltpu.VM...  34.3 us
    pallas_call x1, Pallas kernels, local_stack(): pl.pallas_call(store_kernel, out_shape=[jax.ShapeDtypeStruct((batch, span...  1.16 us

profile of v6, /device:TPU:7, one launch (start us, length us, event | category | flops | bytes accessed | tf_op | source)
XLA Modules:
  0.0 36.1 jit_solution(1754030792458774229)
XLA Ops:
  0.6 34.3 %shard_map.95 = (f32[2,256,512]{2,1,0:T(8,128)S(1)}, f32[2,256,256]{2,1,0:T(8,128)S(1)}) custom-call(bf16[2,256,512]{2,1,0:T(8,128)(2,1)} %signal.1, bf16[2,256,256]{2,1,0:T(8,128)(2,1)} %cond.1, bf16[10,512,1024]{2,1,0:T(8,128)(2,1)} %w_now.1, bf16[10,512,1024]{2,1,0:T(8,128)(2,1)} %w_past.1, bf16[10,256,1024]{2,1,0:T(8,128)(2,1)} %w_cond.1, ...), custom_call_target="tpu_custom_call" | custom-call | tf_op jit(solution)/shard_map/pallas_call | solution.py:314
  34.9 1.2 %shard_map.96 = (f32[2,256,512]{2,1,0:T(8,128)}, f32[2,256,256]{2,1,0:T(8,128)}) custom-call(f32[2,256,512]{2,1,0:T(8,128)S(1)} %get-tuple-element.4.h, f32[2,256,256]{2,1,0:T(8,128)S(1)} %get-tuple-element.5.skip), custom_call_target="tpu_custom_call" | custom-call | tf_op jit(solution)/shard_map/pallas_call | solution.py:343

commit v7 on v6

--- a/solution.py
+++ b/solution.py
@@ -254,21 +254,22 @@
             past = u[s, last, at]
             a = gate(lambda lo, hi: z_part[at, lo:hi] + jnp.dot(past, w_in[last, depth:, lo:hi], preferred_element_type=F32))
             h_out[s, at] = h[s, pl.ds(pl.multiple_of(TILE + part * rows, TILE), rows)] + jnp.dot(a, w_mix[last], preferred_element_type=F32)
-            skip[s, at] += jnp.dot(a, w_sum[last], preferred_element_type=F32)
+            x = jnp.concatenate([acts[s, last - 1, at], a], axis=1)
+            skip[s, at] += jnp.dot(x, w_sum[last - 1:].reshape(2 * ch, skip.shape[2]), preferred_element_type=F32)
             return carry
 
-        lax.fori_loop(0, 2, finish, 0)
+        lax.fori_loop(0, 2, finish, 0, unroll=True)
 
     def sum_skip(s):
         @pl.when(s == 0)
         def _():
             landed(w_sum, sum_sem)
 
-        x = jnp.concatenate([acts[s, k] for k in range(last)], axis=1)
-        skip[s] = jnp.dot(x, w_sum[:last].reshape(last * ch, skip.shape[2]), preferred_element_type=F32)
+        x = jnp.concatenate([acts[s, k] for k in range(last - 1)], axis=1)
+        skip[s] = jnp.dot(x, w_sum[:last - 1].reshape((last - 1) * ch, skip.shape[2]), preferred_element_type=F32)
 
     early = [2 * k for k in range(9)] + [2 * k + 1 for k in range(9)] + [20, 21, 18, 19]
-    late = [0, 2, 4, 6, 1, 3, 5, 7] + [2 * k for k in range(4, 9)] + [2 * k + 1 for k in range(4, 8)] + [20, 18, 17, 21, 19]
+    late = [0, 2, 4, 6, 1, 3, 5, 7] + [2 * k for k in range(4, 9)] + [2 * k + 1 for k in range(4, 8)] + [20, 18, 21, 17, 19]
 
     def run(i, carry):
         code = jnp.where(me < n_sp // 2, at_step(i, early), at_step(i, late))

time: 36.4 us -> 36.2 us (level)
  no operation moved by 1% of the time
where the time goes in v7:
time: 36.2 us; the launch traced here: 36.1 us
  Pallas kernels  35.5 us (98%)
  between operations  0.64 us (2%)
    pallas_call x1, Pallas kernels, local_stack(): pl.pallas_call(functools.partial(stack_kernel, n_sp), out_shape=[pltpu.VM...  34.3 us
    pallas_call x1, Pallas kernels, local_stack(): pl.pallas_call(store_kernel, out_shape=[jax.ShapeDtypeStruct((batch, span...  1.16 us

profile of v7, /device:TPU:7, one launch (start us, length us, event | category | flops | bytes accessed | tf_op | source)
XLA Modules:
  0.0 36.1 jit_solution(15680693810230524269)
XLA Ops:
  0.6 34.3 %shard_map.95 = (f32[2,256,512]{2,1,0:T(8,128)S(1)}, f32[2,256,256]{2,1,0:T(8,128)S(1)}) custom-call(bf16[2,256,512]{2,1,0:T(8,128)(2,1)} %signal.1, bf16[2,256,256]{2,1,0:T(8,128)(2,1)} %cond.1, bf16[10,512,1024]{2,1,0:T(8,128)(2,1)} %w_now.1, bf16[10,512,1024]{2,1,0:T(8,128)(2,1)} %w_past.1, bf16[10,256,1024]{2,1,0:T(8,128)(2,1)} %w_cond.1, ...), custom_call_target="tpu_custom_call" | custom-call | tf_op jit(solution)/shard_map/pallas_call | solution.py:315
  35.0 1.2 %shard_map.96 = (f32[2,256,512]{2,1,0:T(8,128)}, f32[2,256,256]{2,1,0:T(8,128)}) custom-call(f32[2,256,512]{2,1,0:T(8,128)S(1)} %get-tuple-element.4.h, f32[2,256,256]{2,1,0:T(8,128)S(1)} %get-tuple-element.5.skip), custom_call_target="tpu_custom_call" | custom-call | tf_op jit(solution)/shard_map/pallas_call | solution.py:344

commit v8 on v7

--- a/solution.py
+++ b/solution.py
@@ -273,7 +273,7 @@
 
     def run(i, carry):
         code = jnp.where(me < n_sp // 2, at_step(i, early), at_step(i, late))
-        s, layer = code % batch, code // batch
+        s, layer = lax.rem(code, batch), lax.div(code, batch)
 
         lax.cond(layer < last, lambda: step(s, layer),
                  lambda: lax.cond(layer == last, lambda: last_step(s), lambda: sum_skip(s)))

time: 36.2 us -> 36.2 us (level)
  no operation moved by 1% of the time
where the time goes in v8:
time: 36.2 us; the launch traced here: 36.1 us
  Pallas kernels  35.5 us (98%)
  between operations  0.64 us (2%)
    pallas_call x1, Pallas kernels, local_stack(): pl.pallas_call(functools.partial(stack_kernel, n_sp), out_shape=[pltpu.VM...  34.3 us
    pallas_call x1, Pallas kernels, local_stack(): pl.pallas_call(store_kernel, out_shape=[jax.ShapeDtypeStruct((batch, span...  1.16 us

profile of v8, /device:TPU:7, one launch (start us, length us, event | category | flops | bytes accessed | tf_op | source)
XLA Modules:
  0.0 36.1 jit_solution(15884959266200364088)
XLA Ops:
  0.6 34.3 %shard_map.95 = (f32[2,256,512]{2,1,0:T(8,128)S(1)}, f32[2,256,256]{2,1,0:T(8,128)S(1)}) custom-call(bf16[2,256,512]{2,1,0:T(8,128)(2,1)} %signal.1, bf16[2,256,256]{2,1,0:T(8,128)(2,1)} %cond.1, bf16[10,512,1024]{2,1,0:T(8,128)(2,1)} %w_now.1, bf16[10,512,1024]{2,1,0:T(8,128)(2,1)} %w_past.1, bf16[10,256,1024]{2,1,0:T(8,128)(2,1)} %w_cond.1, ...), custom_call_target="tpu_custom_call" | custom-call | tf_op jit(solution)/shard_map/pallas_call | solution.py:315
  34.9 1.2 %shard_map.96 = (f32[2,256,512]{2,1,0:T(8,128)}, f32[2,256,256]{2,1,0:T(8,128)}) custom-call(f32[2,256,512]{2,1,0:T(8,128)S(1)} %get-tuple-element.4.h, f32[2,256,256]{2,1,0:T(8,128)S(1)} %get-tuple-element.5.skip), custom_call_target="tpu_custom_call" | custom-call | tf_op jit(solution)/shard_map/pallas_call | solution.py:344

commit v9 on v8

--- a/solution.py
+++ b/solution.py
@@ -242,6 +242,8 @@
         depth = x.shape[1]
         z_part[...] = jnp.dot(x, w_in[last, :depth], preferred_element_type=F32) + bias[last:, :]
 
+        skip[s] += jnp.dot(acts[s, last - 1], w_sum[last - 1], preferred_element_type=F32)
+
         rows = span // 2
 
         def finish(part, carry):
@@ -254,8 +256,7 @@
             past = u[s, last, at]
             a = gate(lambda lo, hi: z_part[at, lo:hi] + jnp.dot(past, w_in[last, depth:, lo:hi], preferred_element_type=F32))
             h_out[s, at] = h[s, pl.ds(pl.multiple_of(TILE + part * rows, TILE), rows)] + jnp.dot(a, w_mix[last], preferred_element_type=F32)
-            x = jnp.concatenate([acts[s, last - 1, at], a], axis=1)
-            skip[s, at] += jnp.dot(x, w_sum[last - 1:].reshape(2 * ch, skip.shape[2]), preferred_element_type=F32)
+            skip[s, at] += jnp.dot(a, w_sum[last], preferred_element_type=F32)
             return carry
 
         lax.fori_loop(0, 2, finish, 0, unroll=True)

time: 36.2 us -> 36.2 us (level)
  no operation moved by 1% of the time
where the time goes in v9:
time: 36.2 us; the launch traced here: 36.1 us
  Pallas kernels  35.5 us (98%)
  between operations  0.64 us (2%)
    pallas_call x1, Pallas kernels, local_stack(): pl.pallas_call(functools.partial(stack_kernel, n_sp), out_shape=[pltpu.VM...  34.3 us
    pallas_call x1, Pallas kernels, local_stack(): pl.pallas_call(store_kernel, out_shape=[jax.ShapeDtypeStruct((batch, span...  1.16 us

profile of v9, /device:TPU:7, one launch (start us, length us, event | category | flops | bytes accessed | tf_op | source)
XLA Modules:
  0.0 36.1 jit_solution(5439912431127606879)
XLA Ops:
  0.6 34.3 %shard_map.95 = (f32[2,256,512]{2,1,0:T(8,128)S(1)}, f32[2,256,256]{2,1,0:T(8,128)S(1)}) custom-call(bf16[2,256,512]{2,1,0:T(8,128)(2,1)} %signal.1, bf16[2,256,256]{2,1,0:T(8,128)(2,1)} %cond.1, bf16[10,512,1024]{2,1,0:T(8,128)(2,1)} %w_now.1, bf16[10,512,1024]{2,1,0:T(8,128)(2,1)} %w_past.1, bf16[10,256,1024]{2,1,0:T(8,128)(2,1)} %w_cond.1, ...), custom_call_target="tpu_custom_call" | custom-call | tf_op jit(solution)/shard_map/pallas_call | solution.py:316
  34.9 1.2 %shard_map.96 = (f32[2,256,512]{2,1,0:T(8,128)}, f32[2,256,256]{2,1,0:T(8,128)}) custom-call(f32[2,256,512]{2,1,0:T(8,128)S(1)} %get-tuple-element.4.h, f32[2,256,256]{2,1,0:T(8,128)S(1)} %get-tuple-element.5.skip), custom_call_target="tpu_custom_call" | custom-call | tf_op jit(solution)/shard_map/pallas_call | solution.py:345
